TPU v7x, 32 devices: a whole 2x2x4 slice. The times are simulated.
32 devices in a mesh: row: 2 (over y), theta: 4 (over x, core), gz: 4 (over z).
Axes of the slice: x: 2, y: 2, z: 4, core: 2. Of those that a mesh axis runs over, the one named last changes fastest.
Arguments:
- state_start: float32 [6, 8, 128, 1024], P(None, 'row', 'gz', 'theta'), may hold values from -1.2 to 1.2
- state_section: float32 [6, 8, 128, 1024], P(None, 'row', 'gz', 'theta'), may hold values from -1.5 to 4, as said below
- phase: int32 [8, 128, 1024], P('row', 'gz', 'theta'), may hold values 0 or 1
- cutoff: int32 [4], replicated, may hold values from 1 to 63
Outputs:
- state_next: float32 [6, 8, 128, 1024], P(None, 'row', 'gz', 'theta')
Inputs may be any that keep to these rules, and one draw needn't show every extreme that they name: `state_section`: channel 0 (density) lies in 0.5 to 2.0, channels 1 to 3 (momenta) in -1.5 to 1.5, channel 4 (total energy) in 2.5 to 4.0, channel 5 (jet mass density) in 0 to 1.0.
All inputs are finite; a program needn't handle non-finite values. No bound on the sum of `phase` on one device may be relied on, other than what follows from the above.
Results may differ from a plain program's by a relative error of at most 0.0003.
Values sent between devices are 32-bit elements; how exact they have to be, the bound alone decides.
A program may use at most 64 MiB of HBM per device.

v0:
```python
import math

import jax
import jax.numpy as jnp
from jax import lax
from jax.sharding import PartitionSpec as P

NT = 1024
KMODES = 64


split_speed = 10.0
time_step = 0.05
weno_epsilon = 1e-06
liquid_ratio = 4.4
gas_ratio = 1.4
liquid_stiffness = 0.6


def passed_along(value, axis, steps):
    count = lax.axis_size(axis)
    pairs = [(source, (source + steps) % count) for source in range(count)]
    return lax.ppermute(value, axis, pairs)


def with_halo(cells, sides, width):
    for axis, dim in sides:
        count = lax.axis_size(axis)
        head = lax.slice_in_dim(cells, 0, width, axis=dim)
        tail = lax.slice_in_dim(cells, cells.shape[dim] - width, cells.shape[dim], axis=dim)
        cells = jnp.concatenate(
            [
                lax.ppermute(tail, axis, [(i, (i + 1) % count) for i in range(count)]),
                cells,
                lax.ppermute(head, axis, [((i + 1) % count, i) for i in range(count)]),
            ],
            axis=dim,
        )
    return cells


def pressure_of(state, phase):
    density = state[0]
    kinetic = 0.5 * (state[1] * state[1] + state[2] * state[2] + state[3] * state[3]) / density
    liquid = phase == 1
    heat_ratio = jnp.where(liquid, liquid_ratio, gas_ratio)
    stiffness = jnp.where(liquid, liquid_stiffness, 0.0)
    return (heat_ratio - 1.0) * (state[4] - kinetic) - heat_ratio * stiffness


def weno_face(far_left, near_left, centre, near_right, far_right):
    smooth_left = (
        13.0 / 12.0 * (far_left - 2.0 * near_left + centre) ** 2
        + 0.25 * (far_left - 4.0 * near_left + 3.0 * centre) ** 2
    )
    smooth_mid = (
        13.0 / 12.0 * (near_left - 2.0 * centre + near_right) ** 2
        + 0.25 * (near_left - near_right) ** 2
    )
    smooth_right = (
        13.0 / 12.0 * (centre - 2.0 * near_right + far_right) ** 2
        + 0.25 * (3.0 * centre - 4.0 * near_right + far_right) ** 2
    )
    weight_left = 0.1 / (weno_epsilon + smooth_left) ** 2
    weight_mid = 0.6 / (weno_epsilon + smooth_mid) ** 2
    weight_right = 0.3 / (weno_epsilon + smooth_right) ** 2
    weight_sum = weight_left + weight_mid + weight_right
    value_left = (2.0 * far_left - 7.0 * near_left + 11.0 * centre) / 6.0
    value_mid = (-near_left + 5.0 * centre + 2.0 * near_right) / 6.0
    value_right = (2.0 * centre + 5.0 * near_right - far_right) / 6.0
    return (
        weight_left * value_left + weight_mid * value_mid + weight_right * value_right
    ) / weight_sum


def face_fluxes(padded_line, array_axis, component):
    density = padded_line[0]
    velocity = padded_line[component] / density
    pressure_field = padded_line[6]
    conserved = padded_line[:6]
    flux_rows = [conserved[channel] * velocity for channel in range(6)]
    flux_rows[component] = flux_rows[component] + pressure_field
    flux_rows[4] = flux_rows[4] + pressure_field * velocity
    physical = jnp.stack(flux_rows)
    upward = 0.5 * (physical + split_speed * conserved)
    downward = 0.5 * (physical - split_speed * conserved)
    face_count = padded_line.shape[array_axis] - 5

    def shifted(values, offset):
        return lax.slice_in_dim(values, offset, offset + face_count, axis=array_axis)

    upwind_part = weno_face(
        shifted(upward, 0),
        shifted(upward, 1),
        shifted(upward, 2),
        shifted(upward, 3),
        shifted(upward, 4),
    )
    downwind_part = weno_face(
        shifted(downward, 5),
        shifted(downward, 4),
        shifted(downward, 3),
        shifted(downward, 2),
        shifted(downward, 1),
    )
    return upwind_part + downwind_part


def tendency(centre_cells, radial_line, axial_line, azimuth_line, cycle_start):
    cycle_count = centre_cells.shape[1]
    radial_flux = face_fluxes(radial_line, 1, 1)
    axial_flux = face_fluxes(axial_line, 2, 3)
    azimuth_flux = face_fluxes(azimuth_line, 3, 2)
    cycle_index = (cycle_start + lax.iota(jnp.int32, cycle_count + 1)).astype(centre_cells.dtype)
    face_radius = cycle_index[None, :, None, None]
    cell_radius = face_radius[:, :-1] + 0.5
    weighted = face_radius * radial_flux
    div_radial = (weighted[:, 1:] - weighted[:, :-1]) / cell_radius
    div_axial = axial_flux[:, :, 1:] - axial_flux[:, :, :-1]
    angle_step = 2.0 * math.pi / NT
    div_azimuth = (azimuth_flux[..., 1:] - azimuth_flux[..., :-1]) / (cell_radius * angle_step)
    density = centre_cells[0]
    swirl_speed = centre_cells[2] / density
    radius = cell_radius[0]
    source_radial = (centre_cells[2] * swirl_speed + centre_cells[6]) / radius
    source_swirl = -centre_cells[1] * swirl_speed / radius
    zero_field = jnp.zeros_like(density)
    source = jnp.stack(
        [zero_field, source_radial, source_swirl, zero_field, zero_field, zero_field]
    )
    return source - div_radial - div_axial - div_azimuth


def across_axis(partner):
    sign_flip = jnp.array([1.0, -1.0, -1.0, 1.0, 1.0, 1.0, 1.0], partner.dtype)[:, None, None, None]
    return partner[:, ::-1] * sign_flip


def build_table(positions, mode_count, length):
    orders = lax.iota(jnp.int32, mode_count)
    phases = positions[:, None] * orders[None, :] % length
    angles = phases.astype(jnp.float32) * (2.0 * math.pi / length)
    return jnp.concatenate([jnp.cos(angles), jnp.sin(angles)], 1)


def cycle_weights(cutoff, mode_count, length):
    orders = lax.iota(jnp.int32, mode_count)
    mode_scale = jnp.where(orders == 0, 1.0 / length, 2.0 / length)
    kept_modes = orders[None, :] <= cutoff[:, None]
    weight_half = jnp.where(kept_modes, mode_scale[None, :], 0.0)
    return jnp.concatenate([weight_half, weight_half], 1)


def apply_filter(cycle_block, weights, theta_id):
    local_theta = cycle_block.shape[3]
    positions = theta_id * local_theta + lax.iota(jnp.int32, local_theta)
    fourier_table = build_table(positions, KMODES, NT)
    coefficients = jnp.einsum(
        "vizt,tk->vizk", cycle_block, fourier_table, precision=lax.Precision.HIGHEST
    )
    coefficients = lax.psum(coefficients, "theta")
    coefficients = coefficients * weights[None, :, None, :]
    return jnp.einsum("vizk,tk->vizt", coefficients, fourier_table, precision=lax.Precision.HIGHEST)


def shards(state_start, state_section, phase, cutoff):
    row_count = lax.axis_size("row")
    row_id = lax.axis_index("row")
    theta_count = lax.axis_size("theta")
    theta_id = lax.axis_index("theta")
    cycle_count = state_section.shape[1]
    filtered_count = cutoff.shape[0]
    pressure_field = pressure_of(state_section, phase)
    fields = jnp.concatenate([state_section, pressure_field[None]], 0)
    partner = passed_along(fields[:, 0:3], "theta", theta_count // 2)
    mirror = across_axis(partner)
    outer_rim = jnp.repeat(fields[:, -1:], 3, axis=1)
    padded = with_halo(fields, (("row", 1), ("theta", 3), ("gz", 2)), 3)
    radial_line = padded[:, :, 3:-3, 3:-3]
    axial_line = padded[:, 3:-3, :, 3:-3]
    azimuth_line = padded[:, 3:-3, 3:-3, :]
    lower_rim = jnp.where(row_id == 0, mirror, radial_line[:, :3])
    upper_rim = jnp.where(row_id == row_count - 1, outer_rim, radial_line[:, -3:])
    radial_line = jnp.concatenate([lower_rim, fields, upper_rim], 1)
    tendencies = tendency(fields, radial_line, axial_line, azimuth_line, row_id * cycle_count)
    advanced = 0.75 * state_start + 0.25 * (state_section + time_step * tendencies)
    weights = cycle_weights(cutoff, KMODES, NT)
    filtered = apply_filter(advanced, weights, theta_id)
    inner_next = jnp.where(row_id == 0, filtered, advanced)
    return jnp.concatenate([inner_next, advanced[:, filtered_count:]], 1)


def solution(mesh):
    in_specs = (
        P(None, "row", "gz", "theta"),
        P(None, "row", "gz", "theta"),
        P("row", "gz", "theta"),
        P(),
    )
    out_specs = P(None, "row", "gz", "theta")
    return jax.shard_map(shards, mesh=mesh, in_specs=in_specs, out_specs=out_specs, check_vma=False)
```

profile of v0, /device:TPU:0, one launch (start us, length us, event | category | flops | bytes accessed | tf_op | source)
XLA Modules:
  0.0 148.2 jit_solution(16903499594754744437)
XLA Ops:
  6.6 1.4 bitcast_dynamic-update-slice_fusion
  7.9 0.1 copy-done
  8.0 1.2 fusion.11
  9.2 3.0 %collective-permute-start.2 = (f32[7,3,32,256]{3,2,1,0:T(8,128)}, f32[7,3,32,256]{3,2,1,0:T(8,128)S(1)}, u32[]{:S(2)}, u32[]{:S(2)}) collective-permute-start(f32[7,3,32,256]{3,2,1,0:T(8,128)} %get-tuple-element.24), channel_id=1, source_target_pairs={{16,0},{0,16},{17,1},{1,17},{18,2},{2,18},{19,3},{3,19},{20,4},{4,... | collective-permute-start | bytes 2064392 | tf_op jit(solution)/shard_map/ppermute | solution.py:35
  12.2 1.5 %collective-permute-start = (f32[7,3,32,256]{3,2,1,0:T(8,128)}, f32[7,3,32,256]{3,2,1,0:T(8,128)}, u32[]{:S(2)}, u32[]{:S(2)}) collective-permute-start(f32[7,3,32,256]{3,2,1,0:T(8,128)} %get-tuple-element.24), channel_id=1, source_target_pairs={{0,8},{4,12},{8,0},{12,4},{1,9},{5,13},{9,1},{13,5},{2,10},{6,14},... | collective-permute-start | bytes 2064392 | tf_op jit(solution)/shard_map/ppermute | solution.py:23
  13.7 0.5 collective-permute-start.1
  14.2 0.1 divide_dynamic-update-slice_fusion
  14.4 0.0 copy-start.10
  14.4 0.0 copy-start.7
  14.5 0.6 fusion.47
  15.1 13.7 %collective-permute-done.2 = f32[7,3,32,256]{3,2,1,0:T(8,128)S(1)} collective-permute-done((f32[7,3,32,256]{3,2,1,0:T(8,128)}, f32[7,3,32,256]{3,2,1,0:T(8,128)S(1)}, u32[]{:S(2)}, u32[]{:S(2)}) %collective-permute-start.2) | collective-permute-done | bytes 688160 | tf_op jit(solution)/shard_map/ppermute | solution.py:35
  28.7 0.1 broadcast_select_fusion
  28.8 13.8 %collective-permute-done.1 = f32[7,3,32,256]{3,2,1,0:T(8,128)S(1)} collective-permute-done((f32[7,3,32,256]{3,2,1,0:T(8,128)}, f32[7,3,32,256]{3,2,1,0:T(8,128)S(1)}, u32[]{:S(2)}, u32[]{:S(2)}) %collective-permute-start.1) | collective-permute-done | bytes 688160 | tf_op jit(solution)/shard_map/ppermute | solution.py:33
  42.6 0.0 collective-permute-done
  42.6 1.5 %multiply_select_fusion = f32[7,3,32,256]{3,2,1,0:T(8,128)S(1)} fusion(f32[7,3,32,256]{3,2,1,0:T(8,128)S(1)} %collective-permute-done.1, f32[7,3,32,256]{3,2,1,0:T(8,128)} %collective-permute-done, f32[7]{0:T(128)S(1)} %copy-done.10, pred[]{:T(512)S(6)} %eq.25), kind=kLoop, calls=%fused_computation.37 | loop fusion | flops 344064 | bytes 2064413 | tf_op jit(solution)/shard_map/jit(_where)/select_n | solution.py:182
  44.2 1.9 %pad_maximum_fusion.2 = (f32[7,10,32,256]{3,2,1,0:T(8,128)}, f32[7,10,32,256]{3,2,1,0:T(8,128)S(1)}) fusion(f32[7,3,32,256]{3,2,1,0:T(8,128)S(1)} %broadcast_select_fusion, f32[1,4,32,256]{3,2,1,0:T(8,128)S(1)} %bitcast.49, f32[6,4,32,256]{3,2,1,0:T(8,128)S(1)} %copy-done, f32[7,3,32,256]{3,2,1,0:T(8,128)S(1)} %multiply_select_fusion, ...), kind=kLoop, calls=%fused_computation.2 | loop fusion | flops 2867200 | bytes 8257536 | tf_op jit(solution)/shard_map/concatenate | solution.py:184
  46.1 1.8 %fusion.56 = (f32[7,10,32,3]{3,2,1,0:T(8,128)}, f32[7,10,32,3]{3,2,1,0:T(8,128)}) fusion(f32[7,10,32,256]{3,2,1,0:T(8,128)S(1)} %get-tuple-element.22), kind=kLoop, calls=%fused_computation.127 | loop fusion | bytes 107520 | tf_op jit(solution)/shard_map/slice | solution.py:30
  47.9 2.6 %copy.7 = f32[7,10,32,3]{2,0,3,1:T(8,128)} copy(f32[7,10,32,3]{3,2,1,0:T(8,128)} %get-tuple-element.20) | data formatting | bytes 53760 | tf_op jit(solution)/shard_map/slice | solution.py:29
  50.5 0.3 collective-permute-start.4
  50.8 2.4 %copy.6 = f32[7,10,32,3]{2,0,3,1:T(8,128)} copy(f32[7,10,32,3]{3,2,1,0:T(8,128)} %get-tuple-element.19) | data formatting | bytes 53760 | tf_op jit(solution)/shard_map/slice | solution.py:30
  53.2 0.2 collective-permute-start.3
  53.4 0.1 multiply_dynamic-update-slice_fusion
  53.5 0.1 add_dynamic-update-slice_fusion
  53.7 0.1 fusion.16
  53.8 0.7 add_multiply_fusion
  54.5 5.2 %add_multiply_fusion.3 = f32[6,5,32,256]{3,2,1,0:T(8,128)} fusion(f32[6,10,32,256]{3,2,1,0:T(8,128)S(1)} %get-tuple-element.16, f32[6,10,32,256]{3,2,1,0:T(8,128)S(1)} %get-tuple-element.15, f32[5]{0:T(128)S(1)} %add_convert_fusion), kind=kLoop, calls=%fused_computation.20 | loop fusion | flops 31948800 | bytes 10813460 | tf_op jit(solution)/shard_map/mul | solution.py:117
  59.7 1.4 copy.9
  61.1 0.0 collective-permute-done.3
  61.1 1.4 copy.8
  62.5 2.6 %pad_maximum_fusion.1 = f32[7,10,32,262]{3,2,1,0:T(8,128)S(1)} fusion(f32[7,10,32,3]{3,2,1,0:T(8,128)S(1)} %copy.9, f32[7,3,32,256]{3,2,1,0:T(8,128)} %copy-done.3, f32[1,4,32,256]{3,2,1,0:T(8,128)S(1)} %bitcast.50, f32[6,4,32,256]{3,2,1,0:T(8,128)S(1)} %copy-done, f32[7,3,32,256]{3,2,1,0:T(8,128)} %copy-done.1, f32[7,10,32,3]{3,2,1,0:T(8,128)S(1)} %copy.8), kind=kLoop, calls=%fused_computation.1 | loop fusion | flops 2934400 | bytes 4695040 | tf_op jit(solution)/shard_map/concatenate | solution.py:31
  65.1 0.2 fusion.55
  65.2 0.9 copy-done.2
  66.1 0.2 copy-done.4
  66.4 0.2 multiply_dynamic-update-slice_fusion.1
  66.6 0.3 fusion.26
  66.8 0.3 fusion.25
  67.1 0.3 fusion.23
  67.4 0.3 fusion.22
  67.7 0.3 fusion.20
  68.0 0.3 add_multiply_fusion.1
  68.3 3.9 %collective-permute-start.6 = (f32[7,10,3,262]{3,2,1,0:T(4,128)S(1)}, f32[7,10,3,262]{3,2,1,0:T(4,128)S(1)}, u32[]{:S(2)}, u32[]{:S(2)}) collective-permute-start(f32[7,10,3,262]{3,2,1,0:T(4,128)S(1)} %get-tuple-element.18), channel_id=1, source_target_pairs={{1,0},{2,1},{3,2},{0,3},{5,4},{6,5},{7,6},{4,7},{9,8},{10,9},{11,1... | collective-permute-start | bytes 660248 | tf_op jit(solution)/shard_map/ppermute | solution.py:35
  72.2 0.0 collective-permute-start.5
  72.2 5.9 %divide_add_fusion = f32[6,4,32,257]{3,2,1,0:T(8,128)S(1)} fusion(f32[6,4,32,262]{3,2,1,0:T(8,128)S(1)} %get-tuple-element.14, f32[6,4,32,262]{3,2,1,0:T(8,128)S(1)} %get-tuple-element.13), kind=kLoop, calls=%fused_computation.13 | loop fusion | flops 25461504 | bytes 8684544 | tf_op jit(solution)/shard_map/add | solution.py:106
  78.1 4.3 %collective-permute-done.6 = f32[7,10,3,262]{3,2,1,0:T(4,128)S(1)} collective-permute-done((f32[7,10,3,262]{3,2,1,0:T(4,128)S(1)}, f32[7,10,3,262]{3,2,1,0:T(4,128)S(1)}, u32[]{:S(2)}, u32[]{:S(2)}) %collective-permute-start.6) | collective-permute-done | bytes 220112 | tf_op jit(solution)/shard_map/ppermute | solution.py:35
  82.4 10.1 %collective-permute-done.5 = f32[7,10,3,262]{3,2,1,0:T(4,128)S(1)} collective-permute-done((f32[7,10,3,262]{3,2,1,0:T(4,128)S(1)}, f32[7,10,3,262]{3,2,1,0:T(4,128)S(1)}, u32[]{:S(2)}, u32[]{:S(2)}) %collective-permute-start.5) | collective-permute-done | bytes 220112 | tf_op jit(solution)/shard_map/ppermute | solution.py:33
  92.5 5.7 %pad_maximum_fusion = f32[7,10,38,262]{3,2,1,0:T(8,128)S(1)} fusion(f32[7,10,3,262]{3,2,1,0:T(4,128)S(1)} %collective-permute-done.6, f32[7,10,32,3]{3,2,1,0:T(8,128)S(1)} %copy.9, f32[7,3,32,256]{3,2,1,0:T(8,128)S(1)} %copy-done.4, f32[1,4,32,256]{3,2,1,0:T(8,128)S(1)} %bitcast.57, f32[6,4,32,256]{3,2,1,0:T(8,128)S(1)} %copy-done, ...), kind=kLoop, calls=%fused_computation | loop fusion | flops 4878440 | bytes 5575360 | tf_op jit(solution)/shard_map/concatenate | solution.py:31
  98.2 0.2 multiply_dynamic-update-slice_fusion.2
  98.4 0.1 fusion.32
  98.5 0.1 fusion.31
  98.6 0.2 add_dynamic-update-slice_fusion.1
  98.8 0.2 fusion.30
  98.9 0.1 fusion.28
  99.1 0.3 add_multiply_fusion.2
  99.4 0.0 copy-start.8
  99.4 0.0 copy-start.9
  99.4 5.0 %divide_add_fusion.1 = f32[6,4,33,256]{3,2,1,0:T(8,128)S(1)} fusion(f32[6,4,38,256]{3,2,1,0:T(8,128)S(1)} %get-tuple-element.12, f32[6,4,38,256]{3,2,1,0:T(8,128)S(1)} %get-tuple-element.11), kind=kLoop, calls=%fused_computation.17 | loop fusion | flops 26155008 | bytes 8921088 | tf_op jit(solution)/shard_map/add | solution.py:106
  104.5 0.7 fusion.7
  105.2 0.0 copy-start.11
  105.2 1.6 %fusion.48 = f32[6,4,32,128]{3,2,1,0:T(8,128)} fusion(f32[6,4,32,256]{3,2,1,0:T(8,128)S(1)} %fusion.7, f32[256,64]{1,0:T(8,128)S(1)} %get-tuple-element.26, f32[256,64]{1,0:T(8,128)S(1)} %get-tuple-element.25), kind=kOutput, calls=%fused_computation.112 | convolution fusion | flops 302022656 | bytes 1310720 | tf_op jit(solution)/shard_map/vizt,tk->vizk/dot_general | solution.py:158
  106.8 0.0 all-reduce.2.cloned.1.call-update
  106.8 0.1 fusion.49
  106.9 0.1 pad_maximum_fusion.8
  107.0 31.6 %all-reduce.2.cloned.1.call-done = f32[6,4,32,128]{3,2,1,0:T(8,128)} async-done(((f32[6,4,32,128]{3,2,1,0:T(8,128)}), f32[6,4,32,128]{3,2,1,0:T(8,128)}) %all-reduce.2.cloned.1.call-update) | async-done | bytes 393232 | tf_op jit(solution)/shard_map/psum | solution.py:161
  138.6 2.7 %convolution_select_fusion = f32[6,4,32,256]{3,2,1,0:T(8,128)} fusion(f32[6,4,32,256]{3,2,1,0:T(8,128)S(1)} %fusion.7, f32[6,4,32,128]{3,2,1,0:T(8,128)} %all-reduce.2.cloned.1.call-done, pred[]{:T(512)S(6)} %eq.25, f32[4,128]{1,0:T(4,128)S(1)} %pad_maximum_fusion.8, f32[256,64]{1,0:T(8,128)S(1)} %get-tuple-element.26, f32[256,64]{1,0:T(8,128)S(1)} %get-tuple-element.25), kind=kOutput, calls=%fused_computation.9 | convolution fusion | flops 302317568 | bytes 2099201 | tf_op jit(solution)/shard_map/vizk,tk->vizt/dot_general | solution.py:163
  (30 shorter events, 0.3 us)
Async XLA Ops:
  6.5 1.5 copy-start
  6.5 132.1 %all-reduce.2.cloned.1.call-start = ((), (), s32[]{:S(2)}) async-start(), calls=%async_computation | async-start | bytes 786432 | tf_op jit(solution)/shard_map/psum | solution.py:161
  9.2 19.5 %collective-permute-start.2 = (f32[7,3,32,256]{3,2,1,0:T(8,128)}, f32[7,3,32,256]{3,2,1,0:T(8,128)S(1)}, u32[]{:S(2)}, u32[]{:S(2)}) collective-permute-start(f32[7,3,32,256]{3,2,1,0:T(8,128)} %get-tuple-element.24), channel_id=1, source_target_pairs={{16,0},{0,16},{17,1},{1,17},{18,2},{2,18},{19,3},{3,19},{20,4},{4,... | collective-permute-start | bytes 2064392 | tf_op jit(solution)/shard_map/ppermute | solution.py:35
  12.2 30.4 %collective-permute-start = (f32[7,3,32,256]{3,2,1,0:T(8,128)}, f32[7,3,32,256]{3,2,1,0:T(8,128)}, u32[]{:S(2)}, u32[]{:S(2)}) collective-permute-start(f32[7,3,32,256]{3,2,1,0:T(8,128)} %get-tuple-element.24), channel_id=1, source_target_pairs={{0,8},{4,12},{8,0},{12,4},{1,9},{5,13},{9,1},{13,5},{2,10},{6,14},... | collective-permute-start | bytes 2064392 | tf_op jit(solution)/shard_map/ppermute | solution.py:23
  13.7 28.9 %collective-permute-start.1 = (f32[7,3,32,256]{3,2,1,0:T(8,128)}, f32[7,3,32,256]{3,2,1,0:T(8,128)S(1)}, u32[]{:S(2)}, u32[]{:S(2)}) collective-permute-start(f32[7,3,32,256]{3,2,1,0:T(8,128)} %get-tuple-element.23), channel_id=1, source_target_pairs={{0,16},{16,0},{1,17},{17,1},{2,18},{18,2},{3,19},{19,3},{4,20},{20... | collective-permute-start | bytes 2064392 | tf_op jit(solution)/shard_map/ppermute | solution.py:33
  14.4 28.2 %copy-start.10 = (f32[7]{0:T(128)S(1)}, f32[7]{0:T(128)}, u32[]{:S(2)}) copy-start(f32[7]{0:T(128)} %constant.69.clone) | copy-start | bytes 88
  14.4 29.7 %copy-start.7 = (f32[6,4,32,256]{3,2,1,0:T(8,128)}, f32[6,4,32,256]{3,2,1,0:T(8,128)S(1)}, u32[]{:S(2)}) copy-start(f32[6,4,32,256]{3,2,1,0:T(8,128)S(1)} %broadcast_dynamic-update-slice_fusion) | copy-start | bytes 2359300
  28.7 15.4 %copy-start.3 = (f32[7,3,32,256]{3,2,1,0:T(8,128)}, f32[7,3,32,256]{3,2,1,0:T(8,128)S(1)}, u32[]{:S(2)}) copy-start(f32[7,3,32,256]{3,2,1,0:T(8,128)S(1)} %collective-permute-done.2) | copy-start | bytes 2064388
  42.6 3.5 %copy-start.1 = (f32[7,3,32,256]{3,2,1,0:T(8,128)}, f32[7,3,32,256]{3,2,1,0:T(8,128)S(1)}, u32[]{:S(2)}) copy-start(f32[7,3,32,256]{3,2,1,0:T(8,128)S(1)} %collective-permute-done.1) | copy-start | bytes 2064388
  47.9 5.6 %copy-start.5 = (f32[7,10,32,256]{3,2,1,0:T(8,128)S(1)}, f32[7,10,32,256]{3,2,1,0:T(8,128)}, u32[]{:S(2)}) copy-start(f32[7,10,32,256]{3,2,1,0:T(8,128)} %get-tuple-element.21) | copy-start | bytes 6881284
  50.5 9.2 %collective-permute-start.4 = (f32[7,10,32,3]{2,0,3,1:T(8,128)}, f32[7,10,32,3]{2,0,3,1:T(8,128)}, u32[]{:S(2)}, u32[]{:S(2)}) collective-permute-start(f32[7,10,32,3]{2,0,3,1:T(8,128)} %copy.7), channel_id=1, source_target_pairs={{4,0},{8,4},{12,8},{0,12},{5,1},{9,5},{13,9},{1,13},{6,2},{10,6},{... | collective-permute-start | bytes 80648 | tf_op jit(solution)/shard_map/ppermute | solution.py:35
  53.2 7.9 %collective-permute-start.3 = (f32[7,10,32,3]{2,0,3,1:T(8,128)}, f32[7,10,32,3]{2,0,3,1:T(8,128)}, u32[]{:S(2)}, u32[]{:S(2)}) collective-permute-start(f32[7,10,32,3]{2,0,3,1:T(8,128)} %copy.6), channel_id=1, source_target_pairs={{0,4},{4,8},{8,12},{12,0},{1,5},{5,9},{9,13},{13,1},{2,6},{6,10},{... | collective-permute-start | bytes 80648 | tf_op jit(solution)/shard_map/ppermute | solution.py:33
  65.0 1.1 copy-start.2
  65.1 1.3 copy-start.4
  68.3 14.1 %collective-permute-start.6 = (f32[7,10,3,262]{3,2,1,0:T(4,128)S(1)}, f32[7,10,3,262]{3,2,1,0:T(4,128)S(1)}, u32[]{:S(2)}, u32[]{:S(2)}) collective-permute-start(f32[7,10,3,262]{3,2,1,0:T(4,128)S(1)} %get-tuple-element.18), channel_id=1, source_target_pairs={{1,0},{2,1},{3,2},{0,3},{5,4},{6,5},{7,6},{4,7},{9,8},{10,9},{11,1... | collective-permute-start | bytes 660248 | tf_op jit(solution)/shard_map/ppermute | solution.py:35
  72.2 20.3 %collective-permute-start.5 = (f32[7,10,3,262]{3,2,1,0:T(4,128)S(1)}, f32[7,10,3,262]{3,2,1,0:T(4,128)S(1)}, u32[]{:S(2)}, u32[]{:S(2)}) collective-permute-start(f32[7,10,3,262]{3,2,1,0:T(4,128)S(1)} %get-tuple-element.17), channel_id=1, source_target_pairs={{0,1},{1,2},{2,3},{3,0},{4,5},{5,6},{6,7},{7,4},{8,9},{9,10},{10,1... | collective-permute-start | bytes 660248 | tf_op jit(solution)/shard_map/ppermute | solution.py:33
  99.4 5.0 %copy-start.6 = (f32[6,5,32,256]{3,2,1,0:T(8,128)S(1)}, f32[6,5,32,256]{3,2,1,0:T(8,128)}, u32[]{:S(2)}) copy-start(f32[6,5,32,256]{3,2,1,0:T(8,128)} %add_multiply_fusion.3) | copy-start | bytes 2949124
  99.4 5.0 %copy-start.8 = (f32[6,4,32,256]{3,2,1,0:T(8,128)S(1)}, f32[6,4,32,256]{3,2,1,0:T(8,128)}, u32[]{:S(2)}) copy-start(f32[6,4,32,256]{3,2,1,0:T(8,128)} %copy-done.7) | copy-start | bytes 2359300
  99.4 5.0 %copy-start.9 = (f32[6,4,32,256]{3,2,1,0:T(8,128)S(1)}, f32[6,4,32,256]{3,2,1,0:T(8,128)}, u32[]{:S(2)}) copy-start(f32[6,4,32,256]{3,2,1,0:T(8,128)} %param.5) | copy-start | bytes 2359300
  105.2 1.6 %copy-start.11 = (s32[4]{0:T(128)S(1)}, s32[4]{0:T(128)}, u32[]{:S(2)}) copy-start(s32[4]{0:T(128)} %param.8) | copy-start | bytes 52
Sparse Core Ops, SparseCore 0:
  106.9 31.6 all-reduce.1
where the time goes:
time: 149 us; the launch traced here: 148 us
  waiting for transfers between devices  73.5 us (49%)
  other arithmetic  36.1 us (24%)
  between operations  13.8 us (9%)
  local copies, waits for them, and re-layouts  11 us (7%)
  starting transfers between devices  9.39 us (6%)
  matrix products  4.34 us (3%)
    psum x1, waiting for transfers between devices, apply_filter(): coefficients = lax.psum(coefficients, 'theta')  31.6 us
    ppermute x3, waiting for transfers between devices, with_halo(): lax.ppermute(tail, axis, [(i, (i + 1) % count) for i in range(count)])  23.9 us
    ppermute x3, waiting for transfers between devices, with_halo(): lax.ppermute(head, axis, [((i + 1) % count, i) for i in range(count)])  18 us
    add x2, other arithmetic, face_fluxes(): return upwind_part + downwind_part  10.9 us
    concatenate x2, other arithmetic, with_halo(): jnp.concatenate([lax.ppermute(tail, axis, [(i, (i + 1) % count) for i in...  8.27 us
    ppermute x3, starting transfers between devices, with_halo(): lax.ppermute(head, axis, [((i + 1) % count, i) for i in range(count)])  7.17 us
    mul x1, other arithmetic, tendency(): weighted = face_radius * radial_flux  5.18 us
    slice x3, local copies, waits for them, and re-layouts, with_halo(): lax.slice_in_dim(cells, cells.shape[dim] - width, cells.shape[dim], axis=...  4.38 us
  transfers between devices with their start and end apart: 8, of which 5 were waited for; matrix products, arithmetic and copies ran while one was open for 11% of the time, Pallas kernels for 0%

commit v1 on v0

v1 whole, which is shorter than its diff:
```python
import functools
import math

import jax
import jax.numpy as jnp
from jax import lax
from jax.experimental import pallas as pl
from jax.experimental.pallas import tpu as pltpu
from jax.sharding import PartitionSpec as P

KMODES = 64
HALO = 3
LANES = 128
SUB = 8

split_speed = 10.0
time_step = 0.05
weno_epsilon = 1e-06
liquid_ratio = 4.4
gas_ratio = 1.4
liquid_stiffness = 0.6


def pressure_of(state, phase):
    kinetic = 0.5 * (state[1] * state[1] + state[2] * state[2] + state[3] * state[3]) / state[0]
    liquid = phase == 1
    heat_ratio = jnp.where(liquid, liquid_ratio, gas_ratio)
    stiffness = jnp.where(liquid, liquid_stiffness, 0.0)
    return (heat_ratio - 1.0) * (state[4] - kinetic) - heat_ratio * stiffness


def upwind_terms(f, count):
    D = [f[i + 1] - f[i] for i in range(count + 4)]
    G = [0.75 * D[i] for i in range(count + 4)]
    s = [D[i + 1] - D[i] for i in range(count + 3)]
    e = [s[i] - s[i + 1] for i in range(count + 2)]
    q = [s[i] * s[i] + 3.0 * weno_epsilon for i in range(count + 3)]
    out = []
    for m in range(count + 1):
        b0 = q[m] + G[m + 1] * (D[m + 1] + s[m])
        b1 = q[m + 1] + G[m + 1] * D[m + 2]
        b2 = q[m + 2] + G[m + 2] * (D[m + 2] - s[m + 2])
        B0 = b0 * (3.0 * b0)
        B1 = b1 * b1
        B2 = b2 * b2
        B2d = B2 + B2
        numer = B1 * (B2d * e[m] + B0 * e[m + 1])
        denom = B1 * (B2 + B0) + B0 * B2d
        r = pl.reciprocal(denom, approx=True)
        r = r * (2.0 - denom * r)
        out.append(numer * r)
    return out


def line_faces(q, velocity, pressure, component, channel, count):
    cells = count + 6
    flux = []
    for i in range(cells):
        if channel == 4:
            value = (q[i] + pressure(i)) * velocity[i]
        else:
            value = q[i] * velocity[i]
            if channel == component:
                value = value + pressure(i)
        flux.append(value)
    scaled = [split_speed * q[i] for i in range(cells)]
    plus = [flux[i] + scaled[i] for i in range(cells)]
    minus = [flux[i] - scaled[i] for i in range(cells)]
    up = upwind_terms(plus, count)
    down = upwind_terms(minus[::-1], count)[::-1]
    faces = []
    for m in range(count + 1):
        linear = 7.0 * (flux[m + 2] + flux[m + 3]) - (flux[m + 1] + flux[m + 4])
        linear = linear + ((scaled[m + 4] - scaled[m + 1]) - 3.0 * (scaled[m + 3] - scaled[m + 2]))
        faces.append(linear + (up[m] + down[m]))
    return faces


def prepare_kernel(sec, phase, press, bottom, top, zlo, zhi, ft, tlo, thi):
    R, Z, T = press.shape
    for r in range(R):
        press[r] = pressure_of([sec[c, r] for c in range(6)], phase[r])
    for c in range(7):
        def row(r):
            return sec[c, r] if c < 6 else press[r]
        for g in range(HALO):
            bottom[c, g] = row(g)
            top[c, g] = row(R - HALO + g)
        for r in range(R):
            value = row(r)
            zlo[c, r] = value[:HALO]
            zhi[c, r] = value[Z - HALO :]
        per = LANES // Z
        for n in range(R // per):
            block = jnp.concatenate([row(n * per + i) for i in range(per)], 0)
            turned = jnp.transpose(block)
            ft[c, :, n * LANES : (n + 1) * LANES] = turned
            tlo[c, :, n * LANES : (n + 1) * LANES] = turned[:HALO]
            thi[c, :, n * LANES : (n + 1) * LANES] = turned[T - HALO :]


def plane_kernel(angle_step, radius, start, sec, press, zlo, zhi, ft, tlo, thi, out, fz, fe, tt, zt):
    _, R, Z, T = sec.shape
    NL = R * Z
    nl = T // LANES
    for c in range(7):
        for n in range(NL // LANES):
            lanes = slice(n * LANES, (n + 1) * LANES)
            fe[c, n, SUB : SUB + T] = ft[c, :, lanes]
            fe[c, n, SUB - HALO : SUB] = tlo[c, :, lanes]
            fe[c, n, SUB + T : SUB + T + HALO] = thi[c, :, lanes]
        for r in range(R):
            for n in range(nl):
                lanes = slice(n * LANES, (n + 1) * LANES)
                fz[c, r, n, SUB : SUB + Z] = sec[c, r, :, lanes] if c < 6 else press[r, :, lanes]
                fz[c, r, n, SUB - HALO : SUB] = zlo[c, r, :, lanes]
                fz[c, r, n, SUB + Z : SUB + Z + HALO] = zhi[c, r, :, lanes]
    tstride = T // SUB
    chunk = 8
    for lane in range(NL // LANES):

        def theta_chunk(k, carry):
            base = k * chunk

            def at(c, i):
                return fe[c, lane, pl.ds(base + (i + SUB - HALO), SUB, stride=tstride), :]

            velocity = [at(2, i) / at(0, i) for i in range(chunk + 6)]
            for c in range(6):
                q = [at(c, i) for i in range(chunk + 6)]
                faces = line_faces(q, velocity, lambda i: at(6, i), 2, c, chunk)
                for m in range(chunk):
                    tt[c, lane, pl.ds(base + m, SUB, stride=tstride), :] = faces[m + 1] - faces[m]
            return carry

        lax.fori_loop(0, tstride // chunk, theta_chunk, 0)
    zstride = Z // SUB

    def axial(step, carry):
        r = step // nl
        n = step - r * nl

        def at(c, i):
            return fz[c, r, n, pl.ds(i + SUB - HALO, SUB, stride=zstride), :]

        velocity = [at(3, i) / at(0, i) for i in range(zstride + 6)]
        for c in range(6):
            q = [at(c, i) for i in range(zstride + 6)]
            faces = line_faces(q, velocity, lambda i: at(6, i), 3, c, zstride)
            for m in range(zstride):
                zt[c, r, n, pl.ds(m, SUB, stride=zstride), :] = faces[m + 1] - faces[m]
        return carry

    lax.fori_loop(0, R * nl, axial, 0)
    per = LANES // Z
    for c in range(6):
        for n in range(NL // LANES):
            turned = jnp.transpose(tt[c, n])
            for i in range(per):
                r = n * per + i
                cell_radius = radius[r] + 0.5
                axial_part = jnp.concatenate([zt[c, r, m] for m in range(nl)], 1)
                tend = -(1.0 / 12.0) * axial_part - turned[i * Z : (i + 1) * Z] * (
                    1.0 / (12.0 * angle_step * cell_radius)
                )
                if c == 1:
                    tend = tend + (sec[2, r] * sec[2, r] / sec[0, r] + press[r]) / cell_radius
                if c == 2:
                    tend = tend - sec[1, r] * sec[2, r] / (sec[0, r] * cell_radius)
                out[c, r] = 0.75 * start[c, r] + 0.25 * (sec[c, r] + time_step * tend)


def radial_kernel(nf, radius, place, part, sec, press, mirror, lower, upper, table, out, coef, lo, hi):
    _, R, Z, T = sec.shape
    first = place[0] == 1
    last = place[1] == 1
    for c in range(7):
        sign = -1.0 if c in (1, 2) else 1.0
        for g in range(HALO):
            rim = sec[c, R - 1] if c < 6 else press[R - 1]
            lo[c, g] = jnp.where(first, sign * mirror[c, HALO - 1 - g], lower[c, g])
            hi[c, g] = jnp.where(last, rim, upper[c, g])

    def radial(n, carry):
        zs = n // (T // LANES)
        rows = pl.ds(pl.multiple_of(zs * SUB, SUB), SUB)
        lanes = pl.ds(pl.multiple_of((n - zs * (T // LANES)) * LANES, LANES), LANES)

        def at(c, i):
            if i < HALO:
                return lo[c, i, rows, lanes]
            if i >= R + HALO:
                return hi[c, i - R - HALO, rows, lanes]
            return sec[c, i - HALO, rows, lanes] if c < 6 else press[i - HALO, rows, lanes]

        velocity = [at(1, i) / at(0, i) for i in range(R + 6)]
        for c in range(6):
            q = [at(c, i) for i in range(R + 6)]
            faces = line_faces(q, velocity, lambda i: at(6, i), 1, c, R)
            weighted = [radius[i] * faces[i] for i in range(R + 1)]
            for i in range(R):
                scale = 0.25 * time_step / (12.0 * (radius[i] + 0.5))
                out[c, i, rows, lanes] = (
                    part[c, i, rows, lanes] - (weighted[i + 1] - weighted[i]) * scale
                )
        return carry

    lax.fori_loop(0, (Z // SUB) * (T // LANES), radial, 0)
    for c in range(6):
        block = jnp.concatenate([out[c, r] for r in range(nf)], 0)
        coef[c] = jnp.dot(
            block, table[...], preferred_element_type=jnp.float32, precision=lax.Precision.HIGHEST
        )


def inverse_kernel(nf, place, adv, coef, weights, table, out):
    _, R, Z, T = adv.shape
    first = place[0] == 1

    @pl.when(first)
    def _():
        for c in range(6):
            rows = [coef[c, r * Z : (r + 1) * Z] * weights[r : r + 1] for r in range(nf)]
            value = lax.dot_general(
                jnp.concatenate(rows, 0),
                table[...],
                (((1,), (1,)), ((), ())),
                preferred_element_type=jnp.float32,
                precision=lax.Precision.HIGHEST,
            )
            for r in range(nf):
                out[c, r] = value[r * Z : (r + 1) * Z]
            for r in range(nf, R):
                out[c, r] = adv[c, r]

    @pl.when(jnp.logical_not(first))
    def _():
        out[...] = adv[...]


def build_table(positions, mode_count, length):
    orders = lax.iota(jnp.int32, mode_count)
    phases = positions[:, None] * orders[None, :] % length
    angles = phases.astype(jnp.float32) * (2.0 * math.pi / length)
    return jnp.concatenate([jnp.cos(angles), jnp.sin(angles)], 1)


def cycle_weights(cutoff, mode_count, length):
    orders = lax.iota(jnp.int32, mode_count)
    mode_scale = jnp.where(orders == 0, 1.0 / length, 2.0 / length)
    kept_modes = orders[None, :] <= cutoff[:, None]
    weight_half = jnp.where(kept_modes, mode_scale[None, :], 0.0)
    return jnp.concatenate([weight_half, weight_half], 1)


def shape_of(*dims):
    return jax.ShapeDtypeStruct(dims, jnp.float32)


def summed(coef, theta_count, theta_id):
    half = coef.shape[1] // 2
    odd = theta_id % 2 == 1
    swap = [(i, i ^ 1) for i in range(theta_count)]
    low, high = coef[:, :half], coef[:, half:]
    keep = jnp.where(odd, high, low) + lax.ppermute(jnp.where(odd, low, high), "theta", swap)
    distance = 2
    while distance < theta_count:
        keep = keep + lax.ppermute(keep, "theta", [(i, i ^ distance) for i in range(theta_count)])
        distance *= 2
    other = lax.ppermute(keep, "theta", swap)
    return jnp.concatenate([jnp.where(odd, other, keep), jnp.where(odd, keep, other)], 1)


def shards(state_start, state_section, phase, cutoff):
    row_count = lax.axis_size("row")
    row_id = lax.axis_index("row")
    theta_count = lax.axis_size("theta")
    theta_id = lax.axis_index("theta")
    gz_count = lax.axis_size("gz")
    _, R, Z, T = state_section.shape
    NL = R * Z
    nf = cutoff.shape[0]
    length = T * theta_count
    whole = pl.BlockSpec(memory_space=pltpu.VMEM)
    scalar = pl.BlockSpec(memory_space=pltpu.SMEM)
    limit = pltpu.CompilerParams(vmem_limit_bytes=48 * 1024 * 1024)

    press, bottom, top, zlo, zhi, ft, tlo, thi = pl.pallas_call(
        prepare_kernel,
        out_shape=[
            shape_of(R, Z, T),
            shape_of(7, HALO, Z, T),
            shape_of(7, HALO, Z, T),
            shape_of(7, R, HALO, T),
            shape_of(7, R, HALO, T),
            shape_of(7, T, NL),
            shape_of(7, HALO, NL),
            shape_of(7, HALO, NL),
        ],
        in_specs=[whole] * 2,
        out_specs=[whole] * 8,
        compiler_params=limit,
        name="prepare",
    )(state_section, phase)

    def along(value, axis, count, step):
        return lax.ppermute(value, axis, [(i, (i + step) % count) for i in range(count)])

    near_tlo = along(thi, "theta", theta_count, 1)
    near_thi = along(tlo, "theta", theta_count, -1)
    near_zlo = along(zhi, "gz", gz_count, 1)
    near_zhi = along(zlo, "gz", gz_count, -1)
    mirror = lax.ppermute(
        bottom, ("row", "theta"), [(i, (i + theta_count // 2) % theta_count) for i in range(theta_count)]
    )
    lower = lax.ppermute(top, "row", [(i, i + 1) for i in range(row_count - 1)])
    upper = lax.ppermute(bottom, "row", [(i + 1, i) for i in range(row_count - 1)])

    radius = (row_id * R + lax.iota(jnp.int32, R + 1)).astype(jnp.float32)
    place = jnp.stack([row_id == 0, row_id == row_count - 1]).astype(jnp.int32)
    part = pl.pallas_call(
        functools.partial(plane_kernel, 2.0 * math.pi / length),
        out_shape=shape_of(6, R, Z, T),
        in_specs=[scalar] + [whole] * 8,
        out_specs=whole,
        scratch_shapes=[
            pltpu.VMEM((7, R, T // LANES, Z + 2 * SUB, LANES), jnp.float32),
            pltpu.VMEM((7, NL // LANES, T + 2 * SUB, LANES), jnp.float32),
            pltpu.VMEM((6, NL // LANES, T, LANES), jnp.float32),
            pltpu.VMEM((6, R, T // LANES, Z, LANES), jnp.float32),
        ],
        compiler_params=limit,
        cost_estimate=pl.CostEstimate(flops=60_000_000, bytes_accessed=8_000_000, transcendentals=0),
        name="plane",
    )(radius, state_start, state_section, press, near_zlo, near_zhi, ft, near_tlo, near_thi)

    positions = theta_id * T + lax.iota(jnp.int32, T)
    table = build_table(positions, KMODES, length)
    weights = cycle_weights(cutoff, KMODES, length)
    advanced, coef = pl.pallas_call(
        functools.partial(radial_kernel, nf),
        out_shape=[shape_of(6, R, Z, T), shape_of(6, nf * Z, 2 * KMODES)],
        in_specs=[scalar] * 2 + [whole] * 7,
        out_specs=[whole] * 2,
        scratch_shapes=[
            pltpu.VMEM((7, HALO, Z, T), jnp.float32),
            pltpu.VMEM((7, HALO, Z, T), jnp.float32),
        ],
        compiler_params=limit,
        name="radial",
    )(radius, place, part, state_section, press, mirror, lower, upper, table)

    coef = summed(coef, theta_count, theta_id)
    return pl.pallas_call(
        functools.partial(inverse_kernel, nf),
        out_shape=shape_of(6, R, Z, T),
        in_specs=[scalar] + [whole] * 4,
        out_specs=whole,
        compiler_params=limit,
        name="inverse",
    )(place, advanced, coef, weights, table)


def solution(mesh):
    in_specs = (
        P(None, "row", "gz", "theta"),
        P(None, "row", "gz", "theta"),
        P("row", "gz", "theta"),
        P(),
    )
    out_specs = P(None, "row", "gz", "theta")
    return jax.shard_map(shards, mesh=mesh, in_specs=in_specs, out_specs=out_specs, check_vma=False)
```

time: 149 us -> 59.4 us (0.40)
  waiting for transfers between devices: 73.5 us -> 18.8 us
  other arithmetic: 36.1 us -> 1.06 us
  Pallas kernels: 0 us -> 16.9 us
  between operations: 13.8 us -> 0.17 us
  starting transfers between devices: 9.39 us -> 18.8 us
  local copies, waits for them, and re-layouts: 11 us -> 3.35 us
  matrix products: 4.34 us -> 0 us
    psum x1 -> x0, waiting for transfers between devices: 31.6 us -> none  [apply_filter(): coefficients = lax.psum(coefficients, 'theta')]
    ppermute x7 -> x10, waiting for transfers between devices: 41.9 us -> 18.8 us  [the longest x4 9.8 us: along(): lax.ppermute(value, axis, [(i, (i + step) % count) for i in range(count)])]
    pallas_call x0 -> x4, Pallas kernels: none -> 16.9 us  [the longest x1 7.69 us: shards(): pl.pallas_call(functools.partial(plane_kernel, 2.0 * math.pi / length), o...]
    add x4 -> x3, other arithmetic: 11.6 us -> 0.06 us  [the longest x1 0.03 us: summed(): jnp.where(odd, high, low)]
    concatenate x4 -> x2, other arithmetic: 11.4 us -> 0.13 us  [the longest x1 0.1 us: build_table(): return jnp.concatenate([jnp.cos(angles), jnp.sin(angles)], 1)]
    ppermute x7 -> x10, starting transfers between devices: 9.38 us -> 18.8 us  [the longest x1 6.21 us: shards(): lower = lax.ppermute(top, 'row', [(i, i + 1) for i in range(row_count - 1)])]
    slice x4 -> x0, local copies, waits for them, and re-layouts: 6.98 us -> none  [the longest x3 4.38 us: with_halo(): lax.slice_in_dim(cells, cells.shape[dim] - width, cells.shape[dim], axis=...]
    mul x4 -> x0, other arithmetic: 6.53 us -> none  [the longest x1 5.18 us: tendency(): weighted = face_radius * radial_flux]
  transfers between devices with their start and end apart: 8 -> 10, of which waited for: 5 -> 6; matrix products, arithmetic and copies ran while one was open for 11% -> 2% of each run, Pallas kernels for 0% -> 13%
where the time goes in v1:
time: 59.4 us; the launch traced here: 59.2 us
  starting transfers between devices  18.8 us (32%)
  waiting for transfers between devices  18.8 us (32%)
  Pallas kernels  16.9 us (28%)
  local copies, waits for them, and re-layouts  3.35 us (6%)
  other arithmetic  1.06 us (2%)
    ppermute x4, waiting for transfers between devices, along(): lax.ppermute(value, axis, [(i, (i + step) % count) for i in range(count)])  9.8 us
    pallas_call x1, Pallas kernels, shards(): pl.pallas_call(functools.partial(plane_kernel, 2.0 * math.pi / length), o...  7.69 us
    ppermute x1, waiting for transfers between devices, summed(): lax.ppermute(keep, 'theta', [(i, i ^ distance) for i in range(theta_count)])  6.31 us
    ppermute x1, starting transfers between devices, shards(): lower = lax.ppermute(top, 'row', [(i, i + 1) for i in range(row_count - 1)])  6.21 us
    pallas_call x1, Pallas kernels, shards(): pl.pallas_call(functools.partial(radial_kernel, nf), out_shape=[shape_of(...  5.64 us
    ppermute x4, starting transfers between devices, along(): lax.ppermute(value, axis, [(i, (i + step) % count) for i in range(count)])  5.61 us
    ppermute x1, starting transfers between devices, shards(): lax.ppermute(bottom, ('row', 'theta'), [(i, (i + theta_count // 2) % thet...  4.86 us
    unnamed x14, local copies, waits for them, and re-layouts  3.35 us
  transfers between devices with their start and end apart: 10, of which 6 were waited for; matrix products, arithmetic and copies ran while one was open for 2% of the time, Pallas kernels for 13%

profile of v1, /device:TPU:0, one launch (start us, length us, event | category | flops | bytes accessed | tf_op | source)
XLA Modules:
  0.0 59.2 jit_solution(1111954678478044818)
XLA Ops:
  0.0 0.0 copy-start
  0.0 1.1 %copy-done = f32[6,4,32,256]{3,2,1,0:T(8,128)S(1)} copy-done((f32[6,4,32,256]{3,2,1,0:T(8,128)S(1)}, f32[6,4,32,256]{3,2,1,0:T(8,128)}, u32[]{:S(2)}) %copy-start) | copy-done | bytes 786456
  1.1 0.0 copy-start.3
  1.1 0.9 %copy-done.3 = s32[4,32,256]{2,1,0:T(8,128)S(1)} copy-done((s32[4,32,256]{2,1,0:T(8,128)S(1)}, s32[4,32,256]{2,1,0:T(8,128)}, u32[]{:S(2)}) %copy-start.3) | copy-done | bytes 131096
  2.0 0.0 copy-start.1
  2.0 0.0 copy-start.2
  2.0 1.4 %prepare.1 = (f32[4,32,256]{2,1,0:T(8,128)S(1)}, f32[7,3,32,256]{3,2,1,0:T(8,128)}, f32[7,3,32,256]{3,2,1,0:T(8,128)}, f32[7,4,3,256]{3,2,1,0:T(4,128)S(1)}, f32...) custom-call(f32[6,4,32,256]{3,2,1,0:T(8,128)S(1)} %copy-done, ...), custom_call_target="tpu_custom_call" | custom-call | tf_op jit(solution)/shard_map/prepare/pallas_call | solution.py:288
  3.4 0.0 copy-start.4
  3.4 0.6 %copy-done.4 = f32[7,4,3,256]{3,2,1,0:T(4,128)} copy-done((f32[7,4,3,256]{3,2,1,0:T(4,128)}, f32[7,4,3,256]{3,2,1,0:T(4,128)S(1)}, u32[]{:S(2)}) %copy-start.4) | copy-done | bytes 86040
  4.1 0.0 copy-start.5
  4.1 0.7 %copy-done.5 = f32[7,4,3,256]{3,2,1,0:T(4,128)} copy-done((f32[7,4,3,256]{3,2,1,0:T(4,128)}, f32[7,4,3,256]{3,2,1,0:T(4,128)S(1)}, u32[]{:S(2)}) %copy-start.5) | copy-done | bytes 86040
  4.8 4.9 %collective-permute-start.4 = (f32[7,3,32,256]{3,2,1,0:T(8,128)}, f32[7,3,32,256]{3,2,1,0:T(8,128)S(1)}, u32[]{:S(2)}, u32[]{:S(2)}) collective-permute-start(f32[7,3,32,256]{3,2,1,0:T(8,128)} %get-tuple-element.21), channel_id=1, source_target_pairs={{0,8},{4,12},{8,0},{12,4},{1,9},{5,13},{9,1},{13,5},{2,10},{6,14},... | collective-permute-start | bytes 2064392 | tf_op jit(solution)/shard_map/ppermute | solution.py:313
  9.6 1.3 %collective-permute-start.6 = (f32[7,3,32,256]{3,2,1,0:T(8,128)}, f32[7,3,32,256]{3,2,1,0:T(8,128)}, u32[]{:S(2)}, u32[]{:S(2)}) collective-permute-start(f32[7,3,32,256]{3,2,1,0:T(8,128)} %get-tuple-element.21), channel_id=1, source_target_pairs={{16,0},{17,1},{18,2},{19,3},{20,4},{21,5},{22,6},{23,7},{24,8},{25... | collective-permute-start | bytes 2064392 | tf_op jit(solution)/shard_map/ppermute | solution.py:317
  10.9 0.1 collective-permute-start.2
  11.0 1.7 %collective-permute-start.3 = (f32[7,3,128]{2,1,0:T(4,128)S(1)}, f32[7,3,128]{2,1,0:T(4,128)S(1)}, u32[]{:S(2)}, u32[]{:S(2)}) collective-permute-start(f32[7,3,128]{2,1,0:T(4,128)S(1)} %get-tuple-element.20), channel_id=1, source_target_pairs={{0,12},{4,0},{8,4},{12,8},{1,13},{5,1},{9,5},{13,9},{2,14},{6,2},{... | collective-permute-start | bytes 32264 | tf_op jit(solution)/shard_map/ppermute | solution.py:307
  12.7 6.2 %collective-permute-start.5 = (f32[7,3,32,256]{3,2,1,0:T(8,128)}, f32[7,3,32,256]{3,2,1,0:T(8,128)}, u32[]{:S(2)}, u32[]{:S(2)}) collective-permute-start(f32[7,3,32,256]{3,2,1,0:T(8,128)} %get-tuple-element.22), channel_id=1, source_target_pairs={{0,16},{1,17},{2,18},{3,19},{4,20},{5,21},{6,22},{7,23},{8,24},{9,... | collective-permute-start | bytes 2064392 | tf_op jit(solution)/shard_map/ppermute | solution.py:316
  18.9 0.6 fusion.7
  19.5 0.1 pad_maximum_fusion.1.table
  19.7 5.0 %collective-permute-done.2.tlo = f32[7,3,128]{2,1,0:T(4,128)S(1)} collective-permute-done((f32[7,3,128]{2,1,0:T(4,128)S(1)}, f32[7,3,128]{2,1,0:T(4,128)S(1)}, u32[]{:S(2)}, u32[]{:S(2)}) %collective-permute-start.2) | collective-permute-done | bytes 10784 | tf_op jit(solution)/shard_map/ppermute | solution.py:307
  24.7 1.5 %collective-permute-start = (f32[7,4,3,256]{3,2,1,0:T(4,128)}, f32[7,4,3,256]{3,2,1,0:T(4,128)S(1)}, u32[]{:S(2)}, u32[]{:S(2)}) collective-permute-start(f32[7,4,3,256]{3,2,1,0:T(4,128)} %copy-done.5), channel_id=1, source_target_pairs={{0,1},{1,2},{2,3},{3,0},{4,5},{5,6},{6,7},{7,4},{8,9},{9,10},{10,1... | collective-permute-start | bytes 258056 | tf_op jit(solution)/shard_map/ppermute | solution.py:307
  26.2 0.0 collective-permute-done.3.thi
  26.2 2.3 %collective-permute-start.1 = (f32[7,4,3,256]{3,2,1,0:T(4,128)}, f32[7,4,3,256]{3,2,1,0:T(4,128)S(1)}, u32[]{:S(2)}, u32[]{:S(2)}) collective-permute-start(f32[7,4,3,256]{3,2,1,0:T(4,128)} %copy-done.4), channel_id=1, source_target_pairs={{0,3},{1,0},{2,1},{3,2},{4,7},{5,4},{6,5},{7,6},{8,11},{9,8},{10,9... | collective-permute-start | bytes 258056 | tf_op jit(solution)/shard_map/ppermute | solution.py:307
  28.5 0.1 add_convert_fusion.place
  28.6 3.6 %collective-permute-done.zlo = f32[7,4,3,256]{3,2,1,0:T(4,128)S(1)} collective-permute-done((f32[7,4,3,256]{3,2,1,0:T(4,128)}, f32[7,4,3,256]{3,2,1,0:T(4,128)S(1)}, u32[]{:S(2)}, u32[]{:S(2)}) %collective-permute-start) | collective-permute-done | bytes 86048 | tf_op jit(solution)/shard_map/ppermute | solution.py:307
  32.2 1.2 %collective-permute-done.1.zhi = f32[7,4,3,256]{3,2,1,0:T(4,128)S(1)} collective-permute-done((f32[7,4,3,256]{3,2,1,0:T(4,128)}, f32[7,4,3,256]{3,2,1,0:T(4,128)S(1)}, u32[]{:S(2)}, u32[]{:S(2)}) %collective-permute-start.1) | collective-permute-done | bytes 86048 | tf_op jit(solution)/shard_map/ppermute | solution.py:307
  33.4 0.0 copy-done.1
  33.4 0.0 copy-done.2
  33.4 7.7 %plane.1.part = f32[6,4,32,256]{3,2,1,0:T(8,128)S(1)} custom-call(f32[5]{0:T(128)S(1)} %add_convert_fusion.1.radius, f32[6,4,32,256]{3,2,1,0:T(8,128)S(1)} %copy-done.2, f32[6,4,32,256]{3,2,1,0:T(8,128)S(1)} %copy-done.1, f32[4,32,256]{2,1,0:T(8,128)S(1)} %get-tuple-element.15.press, f32[7,4,3,256]{3,2,1,0:T(4,128)S(1)} %collective-permute-done.zlo, ...), custom_call_target="tpu_custom_call" | custom-call | flops 60000000 | bytes 8000000 | tf_op jit(solution)/shard_map/plane/pallas_call | solution.py:321
  41.1 0.0 collective-permute-done.4.mirror
  41.1 0.0 collective-permute-done.6.upper
  41.1 0.0 collective-permute-done.5.lower
  41.1 5.6 %radial.1 = (f32[6,4,32,256]{3,2,1,0:T(8,128)S(1)}, f32[6,128,128]{2,1,0:T(8,128)S(1)}) custom-call(f32[5]{0:T(128)S(1)} %add_convert_fusion.1.radius, s32[2]{0:T(128)S(1)} %add_convert_fusion.place, f32[6,4,32,256]{3,2,1,0:T(8,128)S(1)} %plane.1.part, f32[6,4,32,256]{3,2,1,0:T(8,128)S(1)} %copy-done.1, f32[4,32,256]{2,1,0:T(8,128)S(1)} %get-tuple-element.15.press, ...), custom_call_target="tpu_custom_call" | custom-call | tf_op jit(solution)/shard_map/radial/pallas_call | solution.py:340
  46.8 0.1 collective-permute-start.7
  46.9 1.4 %collective-permute-done.7 = f32[6,64,128]{2,1,0:T(8,128)S(1)} collective-permute-done((f32[6,64,128]{2,1,0:T(8,128)S(1)}, f32[6,64,128]{2,1,0:T(8,128)S(1)}, u32[]{:S(2)}, u32[]{:S(2)}) %collective-permute-start.7) | collective-permute-done | bytes 196640 | tf_op jit(solution)/shard_map/ppermute | solution.py:265
  48.3 0.7 %collective-permute-start.8 = (f32[6,64,128]{2,1,0:T(8,128)S(1)}, f32[6,64,128]{2,1,0:T(8,128)S(1)}, u32[]{:S(2)}, u32[]{:S(2)}) collective-permute-start(f32[6,64,128]{2,1,0:T(8,128)S(1)} %select_add_fusion), channel_id=1, source_target_pairs={{0,8},{4,12},{8,0},{12,4},{1,9},{5,13},{9,1},{13,5},{2,10},{6,14},... | collective-permute-start | bytes 589832 | tf_op jit(solution)/shard_map/ppermute | solution.py:268
  49.0 0.0 copy-start.6
  49.0 6.3 %collective-permute-done.8 = f32[6,64,128]{2,1,0:T(8,128)S(1)} collective-permute-done((f32[6,64,128]{2,1,0:T(8,128)S(1)}, f32[6,64,128]{2,1,0:T(8,128)S(1)}, u32[]{:S(2)}, u32[]{:S(2)}) %collective-permute-start.8) | collective-permute-done | bytes 196640 | tf_op jit(solution)/shard_map/ppermute | solution.py:268
  55.4 0.1 collective-permute-start.9
  55.4 0.0 copy-done.6
  55.5 0.1 fusion.8
  55.5 0.1 pad_maximum_fusion.2.weights
  55.6 1.3 %collective-permute-done.9 = f32[6,64,128]{2,1,0:T(8,128)S(1)} collective-permute-done((f32[6,64,128]{2,1,0:T(8,128)S(1)}, f32[6,64,128]{2,1,0:T(8,128)S(1)}, u32[]{:S(2)}, u32[]{:S(2)}) %collective-permute-start.9) | collective-permute-done | bytes 196640 | tf_op jit(solution)/shard_map/ppermute | solution.py:270
  56.9 2.2 %inverse.1 = f32[6,4,32,256]{3,2,1,0:T(8,128)} custom-call(s32[2]{0:T(128)S(1)} %add_convert_fusion.place, f32[6,4,32,256]{3,2,1,0:T(8,128)S(1)} %get-tuple-element.23.adv, f32[6,128,128]{2,1,0:T(8,128)S(1)} %pad_maximum_fusion.coef, f32[4,128]{1,0:T(4,128)S(1)} %pad_maximum_fusion.2.weights, f32[256,128]{1,0:T(8,128)S(1)} %pad_maximum_fusion.1.table), custom_call_target="tpu_custom_call" | custom-call | tf_op jit(solution)/shard_map/inverse/pallas_call | solution.py:354
  (8 shorter events, 0.2 us)
Async XLA Ops:
  0.0 1.1 %copy-start = (f32[6,4,32,256]{3,2,1,0:T(8,128)S(1)}, f32[6,4,32,256]{3,2,1,0:T(8,128)}, u32[]{:S(2)}) copy-start(f32[6,4,32,256]{3,2,1,0:T(8,128)} %sec.5) | copy-start | bytes 2359300
  1.1 0.9 %copy-start.3 = (s32[4,32,256]{2,1,0:T(8,128)S(1)}, s32[4,32,256]{2,1,0:T(8,128)}, u32[]{:S(2)}) copy-start(s32[4,32,256]{2,1,0:T(8,128)} %phase.1) | copy-start | bytes 393220
  2.0 31.3 %copy-start.1 = (f32[6,4,32,256]{3,2,1,0:T(8,128)S(1)}, f32[6,4,32,256]{3,2,1,0:T(8,128)}, u32[]{:S(2)}) copy-start(f32[6,4,32,256]{3,2,1,0:T(8,128)} %sec.5) | copy-start | bytes 2359300
  2.0 31.3 %copy-start.2 = (f32[6,4,32,256]{3,2,1,0:T(8,128)S(1)}, f32[6,4,32,256]{3,2,1,0:T(8,128)}, u32[]{:S(2)}) copy-start(f32[6,4,32,256]{3,2,1,0:T(8,128)} %start.1) | copy-start | bytes 2359300
  3.4 0.6 %copy-start.4 = (f32[7,4,3,256]{3,2,1,0:T(4,128)}, f32[7,4,3,256]{3,2,1,0:T(4,128)S(1)}, u32[]{:S(2)}) copy-start(f32[7,4,3,256]{3,2,1,0:T(4,128)S(1)} %get-tuple-element.17) | copy-start | bytes 258052
  4.1 0.7 %copy-start.5 = (f32[7,4,3,256]{3,2,1,0:T(4,128)}, f32[7,4,3,256]{3,2,1,0:T(4,128)S(1)}, u32[]{:S(2)}) copy-start(f32[7,4,3,256]{3,2,1,0:T(4,128)S(1)} %get-tuple-element.16) | copy-start | bytes 258052
  4.8 36.3 %collective-permute-start.4 = (f32[7,3,32,256]{3,2,1,0:T(8,128)}, f32[7,3,32,256]{3,2,1,0:T(8,128)S(1)}, u32[]{:S(2)}, u32[]{:S(2)}) collective-permute-start(f32[7,3,32,256]{3,2,1,0:T(8,128)} %get-tuple-element.21), channel_id=1, source_target_pairs={{0,8},{4,12},{8,0},{12,4},{1,9},{5,13},{9,1},{13,5},{2,10},{6,14},... | collective-permute-start | bytes 2064392 | tf_op jit(solution)/shard_map/ppermute | solution.py:313
  9.6 31.5 %collective-permute-start.6 = (f32[7,3,32,256]{3,2,1,0:T(8,128)}, f32[7,3,32,256]{3,2,1,0:T(8,128)}, u32[]{:S(2)}, u32[]{:S(2)}) collective-permute-start(f32[7,3,32,256]{3,2,1,0:T(8,128)} %get-tuple-element.21), channel_id=1, source_target_pairs={{16,0},{17,1},{18,2},{19,3},{20,4},{21,5},{22,6},{23,7},{24,8},{25... | collective-permute-start | bytes 2064392 | tf_op jit(solution)/shard_map/ppermute | solution.py:317
  10.9 13.8 %collective-permute-start.2 = (f32[7,3,128]{2,1,0:T(4,128)S(1)}, f32[7,3,128]{2,1,0:T(4,128)S(1)}, u32[]{:S(2)}, u32[]{:S(2)}) collective-permute-start(f32[7,3,128]{2,1,0:T(4,128)S(1)} %get-tuple-element.19), channel_id=1, source_target_pairs={{0,4},{4,8},{8,12},{12,0},{1,5},{5,9},{9,13},{13,1},{2,6},{6,10},{... | collective-permute-start | bytes 32264 | tf_op jit(solution)/shard_map/ppermute | solution.py:307
  11.0 15.3 %collective-permute-start.3 = (f32[7,3,128]{2,1,0:T(4,128)S(1)}, f32[7,3,128]{2,1,0:T(4,128)S(1)}, u32[]{:S(2)}, u32[]{:S(2)}) collective-permute-start(f32[7,3,128]{2,1,0:T(4,128)S(1)} %get-tuple-element.20), channel_id=1, source_target_pairs={{0,12},{4,0},{8,4},{12,8},{1,13},{5,1},{9,5},{13,9},{2,14},{6,2},{... | collective-permute-start | bytes 32264 | tf_op jit(solution)/shard_map/ppermute | solution.py:307
  12.7 28.4 %collective-permute-start.5 = (f32[7,3,32,256]{3,2,1,0:T(8,128)}, f32[7,3,32,256]{3,2,1,0:T(8,128)}, u32[]{:S(2)}, u32[]{:S(2)}) collective-permute-start(f32[7,3,32,256]{3,2,1,0:T(8,128)} %get-tuple-element.22), channel_id=1, source_target_pairs={{0,16},{1,17},{2,18},{3,19},{4,20},{5,21},{6,22},{7,23},{8,24},{9,... | collective-permute-start | bytes 2064392 | tf_op jit(solution)/shard_map/ppermute | solution.py:316
  24.7 7.5 %collective-permute-start = (f32[7,4,3,256]{3,2,1,0:T(4,128)}, f32[7,4,3,256]{3,2,1,0:T(4,128)S(1)}, u32[]{:S(2)}, u32[]{:S(2)}) collective-permute-start(f32[7,4,3,256]{3,2,1,0:T(4,128)} %copy-done.5), channel_id=1, source_target_pairs={{0,1},{1,2},{2,3},{3,0},{4,5},{5,6},{6,7},{7,4},{8,9},{9,10},{10,1... | collective-permute-start | bytes 258056 | tf_op jit(solution)/shard_map/ppermute | solution.py:307
  26.2 7.1 %collective-permute-start.1 = (f32[7,4,3,256]{3,2,1,0:T(4,128)}, f32[7,4,3,256]{3,2,1,0:T(4,128)S(1)}, u32[]{:S(2)}, u32[]{:S(2)}) collective-permute-start(f32[7,4,3,256]{3,2,1,0:T(4,128)} %copy-done.4), channel_id=1, source_target_pairs={{0,3},{1,0},{2,1},{3,2},{4,7},{5,4},{6,5},{7,6},{8,11},{9,8},{10,9... | collective-permute-start | bytes 258056 | tf_op jit(solution)/shard_map/ppermute | solution.py:307
  46.8 1.5 %collective-permute-start.7 = (f32[6,64,128]{2,1,0:T(8,128)S(1)}, f32[6,64,128]{2,1,0:T(8,128)S(1)}, u32[]{:S(2)}, u32[]{:S(2)}) collective-permute-start(f32[6,64,128]{2,1,0:T(8,128)S(1)} %slice_select_fusion), channel_id=1, source_target_pairs={{0,4},{4,0},{8,12},{12,8},{1,5},{5,1},{9,13},{13,9},{2,6},{6,2},{1... | collective-permute-start | bytes 589832 | tf_op jit(solution)/shard_map/ppermute | solution.py:265
  48.3 7.0 %collective-permute-start.8 = (f32[6,64,128]{2,1,0:T(8,128)S(1)}, f32[6,64,128]{2,1,0:T(8,128)S(1)}, u32[]{:S(2)}, u32[]{:S(2)}) collective-permute-start(f32[6,64,128]{2,1,0:T(8,128)S(1)} %select_add_fusion), channel_id=1, source_target_pairs={{0,8},{4,12},{8,0},{12,4},{1,9},{5,13},{9,1},{13,5},{2,10},{6,14},... | collective-permute-start | bytes 589832 | tf_op jit(solution)/shard_map/ppermute | solution.py:268
  49.0 6.4 %copy-start.6 = (s32[4]{0:T(128)S(1)}, s32[4]{0:T(128)}, u32[]{:S(2)}) copy-start(s32[4]{0:T(128)} %param.7) | copy-start | bytes 52
  55.4 1.5 %collective-permute-start.9 = (f32[6,64,128]{2,1,0:T(8,128)S(1)}, f32[6,64,128]{2,1,0:T(8,128)S(1)}, u32[]{:S(2)}, u32[]{:S(2)}) collective-permute-start(f32[6,64,128]{2,1,0:T(8,128)S(1)} %add.39), channel_id=1, source_target_pairs={{0,4},{4,0},{8,12},{12,8},{1,5},{5,1},{9,13},{13,9},{2,6},{6,2},{1... | collective-permute-start | bytes 589832 | tf_op jit(solution)/shard_map/ppermute | solution.py:270

commit v2 on v1

v2 whole, which is shorter than its diff:
```python
import functools
import math

import jax
import jax.numpy as jnp
from jax import lax
from jax.experimental import pallas as pl
from jax.experimental.pallas import tpu as pltpu
from jax.sharding import PartitionSpec as P

KMODES = 64
HALO = 3
LANES = 128
SUB = 8

split_speed = 10.0
time_step = 0.05
weno_epsilon = 1e-06
liquid_ratio = 4.4
gas_ratio = 1.4
liquid_stiffness = 0.6


def pressure_of(state, phase):
    kinetic = 0.5 * (state[1] * state[1] + state[2] * state[2] + state[3] * state[3]) / state[0]
    liquid = phase == 1
    heat_ratio = jnp.where(liquid, liquid_ratio, gas_ratio)
    stiffness = jnp.where(liquid, liquid_stiffness, 0.0)
    return (heat_ratio - 1.0) * (state[4] - kinetic) - heat_ratio * stiffness


def upwind_terms(f, count):
    D = [f[i + 1] - f[i] for i in range(count + 4)]
    G = [0.75 * D[i] for i in range(count + 4)]
    s = [D[i + 1] - D[i] for i in range(count + 3)]
    e = [s[i] - s[i + 1] for i in range(count + 2)]
    q = [s[i] * s[i] + 3.0 * weno_epsilon for i in range(count + 3)]
    out = []
    for m in range(count + 1):
        b0 = q[m] + G[m + 1] * (D[m + 1] + s[m])
        b1 = q[m + 1] + G[m + 1] * D[m + 2]
        b2 = q[m + 2] + G[m + 2] * (D[m + 2] - s[m + 2])
        B0 = b0 * (3.0 * b0)
        B1 = b1 * b1
        B2 = b2 * b2
        B2d = B2 + B2
        numer = B1 * (B2d * e[m] + B0 * e[m + 1])
        denom = B1 * (B2 + B0) + B0 * B2d
        r = pl.reciprocal(denom, approx=True)
        r = r * (2.0 - denom * r)
        out.append(numer * r)
    return out


def line_faces(q, velocity, pressure, component, channel, count):
    cells = count + 6
    flux = []
    for i in range(cells):
        if channel == 4:
            value = (q[i] + pressure(i)) * velocity[i]
        else:
            value = q[i] * velocity[i]
            if channel == component:
                value = value + pressure(i)
        flux.append(value)
    scaled = [split_speed * q[i] for i in range(cells)]
    plus = [flux[i] + scaled[i] for i in range(cells)]
    minus = [flux[i] - scaled[i] for i in range(cells)]
    up = upwind_terms(plus, count)
    down = upwind_terms(minus[::-1], count)[::-1]
    faces = []
    for m in range(count + 1):
        linear = 7.0 * (flux[m + 2] + flux[m + 3]) - (flux[m + 1] + flux[m + 4])
        linear = linear + ((scaled[m + 4] - scaled[m + 1]) - 3.0 * (scaled[m + 3] - scaled[m + 2]))
        faces.append(linear + (up[m] + down[m]))
    return faces


def fused_kernel(
    nf, angle_step, counts, radius, start, sec, phase, table, out, coef,
    press, fz, zph, fe, tt, zt, lo, loph, hi, hiph, own, got, half, cross, whole_sum,
    lo_send, lo_recv, hi_send, hi_recv, z_send, z_recv, t_send, t_recv, c_send, c_recv,
):
    row_count, theta_count, gz_count = counts
    _, R, Z, T = sec.shape
    NL = R * Z
    nl = T // LANES
    per = LANES // Z
    chunks = Z // SUB
    row = lax.axis_index("row")
    theta = lax.axis_index("theta")
    gz = lax.axis_index("gz")
    first = row == 0
    last = row == row_count - 1
    MESH = pl.DeviceIdType.MESH

    right = lax.rem(theta + 1, theta_count)
    left = lax.rem(theta + theta_count - 1, theta_count)
    across = lax.rem(theta + theta_count // 2, theta_count)
    ahead = lax.rem(gz + 1, gz_count)
    behind = lax.rem(gz + gz_count - 1, gz_count)
    odd = lax.rem(theta, 2)
    pair = theta + 1 - 2 * odd

    barrier = pltpu.get_barrier_semaphore()

    def greet(**axes):
        pl.semaphore_signal(barrier, inc=1, device_id=axes, device_id_type=MESH)

    for t in (right, left, across):
        greet(theta=t)
    greet(gz=ahead)
    greet(gz=behind)

    @pl.when(jnp.logical_not(first))
    def _():
        greet(row=row - 1)

    @pl.when(jnp.logical_not(last))
    def _():
        greet(row=row + 1)

    @pl.when(jnp.logical_or(first, last))
    def _():
        pl.semaphore_wait(barrier, 6)

    if row_count > 2:

        @pl.when(jnp.logical_not(jnp.logical_or(first, last)))
        def _():
            pl.semaphore_wait(barrier, 7)

    def remote(src, dst, send, recv, axes):
        return pltpu.make_async_remote_copy(
            src_ref=src, dst_ref=dst, send_sem=send, recv_sem=recv, device_id=axes, device_id_type=MESH
        )

    def slab(k, g0, to, toph, send, recv, axes):
        zs = pl.ds(k * SUB, SUB)
        return (
            remote(sec.at[:, pl.ds(g0, HALO), zs], to.at[:, :, zs], send.at[k, 0], recv.at[k, 0], axes),
            remote(phase.at[pl.ds(g0, HALO), zs], toph.at[:, zs], send.at[k, 1], recv.at[k, 1], axes),
        )

    def mirrored(k):
        return slab(k, 0, lo, loph, lo_send, lo_recv, dict(theta=across))

    def upward(k):
        return slab(k, R - HALO, lo, loph, lo_send, lo_recv, dict(row=row + 1))

    def downward(k):
        return slab(k, 0, hi, hiph, hi_send, hi_recv, dict(row=row - 1))

    def start_all(copies):
        for copy in copies:
            copy.start()

    def mirror_start(k):
        @pl.when(first)
        def _():
            start_all(mirrored(k))

    mirror_start(0)

    def upward_from(k):
        zs = pl.ds(k * SUB, SUB)
        g0 = R - HALO
        axes = dict(row=row + 1)
        return (
            remote(sec.at[:, pl.ds(g0, HALO), zs], lo.at[:, :, zs], c_send.at[k, 3], lo_recv.at[k, 0], axes),
            remote(phase.at[pl.ds(g0, HALO), zs], loph.at[:, zs], c_send.at[k, 4], lo_recv.at[k, 1], axes),
        )

    for k in range(chunks):

        @pl.when(jnp.logical_not(last))
        def _():
            start_all(upward_from(k))

        @pl.when(jnp.logical_not(first))
        def _():
            start_all(downward(k))

    def axial_copies():
        out = []
        for n in range(nl):
            lanes = pl.ds(n * LANES, LANES)
            for side, (src0, dst0, axes) in enumerate(
                ((Z - SUB, 0, dict(gz=ahead)), (0, SUB + Z, dict(gz=behind)))
            ):
                rows = pl.ds(src0, SUB)
                out.append(
                    remote(
                        sec.at[:, :, rows, lanes],
                        fz.at[pl.ds(0, 6), :, n, pl.ds(dst0, SUB)],
                        z_send.at[n, side, 0],
                        z_recv.at[n, side, 0],
                        axes,
                    )
                )
                out.append(
                    remote(
                        phase.at[:, rows, lanes],
                        zph.at[:, n, side],
                        z_send.at[n, side, 1],
                        z_recv.at[n, side, 1],
                        axes,
                    )
                )
        return out

    start_all(axial_copies())

    for r in range(R):
        press[r] = pressure_of([sec[c, r] for c in range(6)], phase[r])

    def field(c, r):
        return sec[c, r] if c < 6 else press[r]

    for c in range(7):
        for n in range(NL // LANES):
            block = jnp.concatenate([field(c, n * per + i) for i in range(per)], 0)
            fe[c, n, SUB : SUB + T] = jnp.transpose(block)
    for c in range(7):
        for r in range(R):
            value = field(c, r)
            for n in range(nl):
                fz[c, r, n, SUB : SUB + Z] = value[:, n * LANES : (n + 1) * LANES]

    def theta_copies():
        return (
            remote(
                fe.at[:, :, pl.ds(T, SUB)], fe.at[:, :, pl.ds(0, SUB)], t_send.at[0], t_recv.at[0], dict(theta=right)
            ),
            remote(
                fe.at[:, :, pl.ds(SUB, SUB)],
                fe.at[:, :, pl.ds(SUB + T, SUB)],
                t_send.at[1],
                t_recv.at[1],
                dict(theta=left),
            ),
        )

    start_all(theta_copies())
    for k in range(1, chunks):
        mirror_start(k)

    tstride = T // SUB
    chunk = SUB
    pieces = tstride // chunk

    def theta_piece(lane, k):
        base = k * chunk

        def at(c, i):
            return fe[c, lane, pl.ds(base + (i + SUB - HALO), SUB, stride=tstride), :]

        velocity = [at(2, i) / at(0, i) for i in range(chunk + 6)]
        for c in range(6):
            q = [at(c, i) for i in range(chunk + 6)]
            faces = line_faces(q, velocity, lambda i: at(6, i), 2, c, chunk)
            for m in range(chunk):
                tt[c, lane, pl.ds(base + m, SUB, stride=tstride), :] = faces[m + 1] - faces[m]

    for lane in range(NL // LANES):

        @pl.loop(1, pieces - 1)
        def _(k):
            theta_piece(lane, k)

    for copy in theta_copies():
        copy.wait()
    for lane in range(NL // LANES):

        @pl.loop(0, 2)
        def _(k):
            theta_piece(lane, k * (pieces - 1))

    for copy in axial_copies():
        copy.wait()
    for side, row0 in enumerate((0, SUB + Z)):
        for r in range(R):
            for n in range(nl):
                cells = [fz[c, r, n, row0 : row0 + SUB] for c in range(6)]
                fz[6, r, n, row0 : row0 + SUB] = pressure_of(cells, zph[r, n, side])
    zstride = Z // SUB

    @pl.loop(0, R * nl)
    def _(step):
        r = step // nl
        n = step - r * nl

        def at(c, i):
            return fz[c, r, n, pl.ds(i + SUB - HALO, SUB, stride=zstride), :]

        velocity = [at(3, i) / at(0, i) for i in range(zstride + 6)]
        for c in range(6):
            q = [at(c, i) for i in range(zstride + 6)]
            faces = line_faces(q, velocity, lambda i: at(6, i), 3, c, zstride)
            for m in range(zstride):
                zt[c, r, n, pl.ds(m, SUB, stride=zstride), :] = faces[m + 1] - faces[m]

    for c in range(6):
        for n in range(NL // LANES):
            turned = jnp.transpose(tt[c, n])
            for i in range(per):
                r = n * per + i
                cell_radius = radius[r] + 0.5
                axial_part = jnp.concatenate([zt[c, r, m] for m in range(nl)], 1)
                tend = -(1.0 / 12.0) * axial_part - turned[i * Z : (i + 1) * Z] * (
                    1.0 / (12.0 * angle_step * cell_radius)
                )
                if c == 1:
                    tend = tend + (sec[2, r] * sec[2, r] / sec[0, r] + press[r]) / cell_radius
                if c == 2:
                    tend = tend - sec[1, r] * sec[2, r] / (sec[0, r] * cell_radius)
                out[c, r] = 0.75 * start[c, r] + 0.25 * (sec[c, r] + time_step * tend)

    @pl.when(last)
    def _():
        for g in range(HALO):
            for c in range(6):
                hi[c, g] = sec[c, R - 1]
            hiph[g] = phase[R - 1]

    sign = jnp.where(first, -1.0, 1.0).astype(jnp.float32)

    def radial_chunk(k):
        rows = pl.ds(k * SUB, SUB)

        @pl.loop(0, nl)
        def _(n):
            lanes = pl.ds(pl.multiple_of(n * LANES, LANES), LANES)
            ghosts = {}
            for i in range(HALO):
                g = jnp.where(first, HALO - 1 - i, i)
                cells = [lo[c, g, rows, lanes] for c in range(6)]
                cells = [sign * v if c in (1, 2) else v for c, v in enumerate(cells)]
                ghosts[i] = cells + [pressure_of(cells, loph[g, rows, lanes])]
                cells = [hi[c, i, rows, lanes] for c in range(6)]
                ghosts[R + HALO + i] = cells + [pressure_of(cells, hiph[i, rows, lanes])]

            def at(c, i):
                if i in ghosts:
                    return ghosts[i][c]
                return sec[c, i - HALO, rows, lanes] if c < 6 else press[i - HALO, rows, lanes]

            velocity = [at(1, i) / at(0, i) for i in range(R + 6)]
            for c in range(6):
                q = [at(c, i) for i in range(R + 6)]
                faces = line_faces(q, velocity, lambda i: at(6, i), 1, c, R)
                weighted = [radius[i] * faces[i] for i in range(R + 1)]
                for i in range(R):
                    scale = 0.25 * time_step / (12.0 * (radius[i] + 0.5))
                    out[c, i, rows, lanes] = out[c, i, rows, lanes] - (weighted[i + 1] - weighted[i]) * scale

    channels = 3
    mine = pl.ds(channels * odd, channels)
    theirs = pl.ds(channels * (1 - odd), channels)

    def swap(k):
        return remote(own.at[k, theirs], got.at[k], c_send.at[k, 0], c_recv.at[k, 0], dict(theta=pair))

    def cross_over(k):
        return remote(half.at[k], cross.at[k], c_send.at[k, 1], c_recv.at[k, 1], dict(theta=across))

    def swap_back(k):
        return remote(
            whole_sum.at[k, mine], whole_sum.at[k, mine], c_send.at[k, 2], c_recv.at[k, 2], dict(theta=pair)
        )

    def stage_a(k):
        rows = slice(k * SUB, (k + 1) * SUB)
        block = jnp.concatenate([out[c, r, rows] for c in range(6) for r in range(nf)], 0)
        value = jnp.dot(block, table[...], preferred_element_type=jnp.float32, precision=lax.Precision.HIGHEST)
        own[k] = value.reshape(6, nf * SUB, value.shape[1])
        swap(k).start()

    def stage_b(k):
        swap(k).wait()
        half[k] = own[k, mine] + got[k]
        cross_over(k).start()

    def stage_c(k):
        cross_over(k).wait()
        whole_sum[k, mine] = half[k] + cross[k]
        swap_back(k).start()

    for k in range(chunks + 2):
        if k < chunks:

            @pl.when(first)
            def _():
                for copy in mirrored(k):
                    copy.wait()

            @pl.when(jnp.logical_not(first))
            def _():
                for copy in upward(k):
                    copy.wait_recv()

            @pl.when(jnp.logical_not(last))
            def _():
                for copy in downward(k):
                    copy.wait_recv()

            radial_chunk(k)

        @pl.when(first)
        def _():
            if k < chunks:
                stage_a(k)
            if 0 <= k - 1 < chunks:
                stage_b(k - 1)
            if 0 <= k - 2 < chunks:
                stage_c(k - 2)

    @pl.when(first)
    def _():
        for k in range(chunks):
            swap_back(k).wait()
            coef[k] = whole_sum[k]

    for k in range(chunks):

        @pl.when(jnp.logical_not(last))
        def _():
            for copy in upward_from(k):
                copy.wait_send()

        @pl.when(jnp.logical_not(first))
        def _():
            for copy in downward(k):
                copy.wait_send()


def inverse_kernel(nf, place, adv, coef, weights, table, out):
    _, R, Z, T = adv.shape
    first = place[0] == 1

    @pl.when(first)
    def _():
        for k in range(Z // SUB):
            rows = [
                coef[k, c, r * SUB : (r + 1) * SUB] * weights[r : r + 1] for c in range(6) for r in range(nf)
            ]
            value = lax.dot_general(
                jnp.concatenate(rows, 0),
                table[...],
                (((1,), (1,)), ((), ())),
                preferred_element_type=jnp.float32,
                precision=lax.Precision.HIGHEST,
            )
            for c in range(6):
                for r in range(nf):
                    at = (c * nf + r) * SUB
                    out[c, r, k * SUB : (k + 1) * SUB] = value[at : at + SUB]
        for c in range(6):
            for r in range(nf, R):
                out[c, r] = adv[c, r]

    @pl.when(jnp.logical_not(first))
    def _():
        out[...] = adv[...]


def build_table(positions, mode_count, length):
    orders = lax.iota(jnp.int32, mode_count)
    phases = positions[:, None] * orders[None, :] % length
    angles = phases.astype(jnp.float32) * (2.0 * math.pi / length)
    return jnp.concatenate([jnp.cos(angles), jnp.sin(angles)], 1)


def cycle_weights(cutoff, mode_count, length):
    orders = lax.iota(jnp.int32, mode_count)
    mode_scale = jnp.where(orders == 0, 1.0 / length, 2.0 / length)
    kept_modes = orders[None, :] <= cutoff[:, None]
    weight_half = jnp.where(kept_modes, mode_scale[None, :], 0.0)
    return jnp.concatenate([weight_half, weight_half], 1)


def shape_of(*dims):
    return jax.ShapeDtypeStruct(dims, jnp.float32)


def shards(state_start, state_section, phase, cutoff):
    row_count = lax.axis_size("row")
    row_id = lax.axis_index("row")
    theta_count = lax.axis_size("theta")
    theta_id = lax.axis_index("theta")
    gz_count = lax.axis_size("gz")
    _, R, Z, T = state_section.shape
    NL = R * Z
    nf = cutoff.shape[0]
    nl = T // LANES
    chunks = Z // SUB
    length = T * theta_count
    whole = pl.BlockSpec(memory_space=pltpu.VMEM)
    scalar = pl.BlockSpec(memory_space=pltpu.SMEM)

    radius = (row_id * R + lax.iota(jnp.int32, R + 1)).astype(jnp.float32)
    place = jnp.stack([row_id == 0, row_id == row_count - 1]).astype(jnp.int32)
    positions = theta_id * T + lax.iota(jnp.int32, T)
    table = build_table(positions, KMODES, length)
    weights = cycle_weights(cutoff, KMODES, length)
    ways = 2 * KMODES

    def vmem(*dims):
        return pltpu.VMEM(dims, jnp.float32)

    def dma(*dims):
        return pltpu.SemaphoreType.DMA(dims)

    advanced, coef = pl.pallas_call(
        functools.partial(fused_kernel, nf, 2.0 * math.pi / length, (row_count, theta_count, gz_count)),
        out_shape=[shape_of(6, R, Z, T), shape_of(chunks, 6, nf * SUB, ways)],
        in_specs=[scalar] + [whole] * 4,
        out_specs=[whole] * 2,
        scratch_shapes=[
            vmem(R, Z, T),
            vmem(7, R, nl, Z + 2 * SUB, LANES),
            pltpu.VMEM((R, nl, 2, SUB, LANES), jnp.int32),
            vmem(7, NL // LANES, T + 2 * SUB, LANES),
            vmem(6, NL // LANES, T, LANES),
            vmem(6, R, nl, Z, LANES),
            vmem(6, HALO, Z, T),
            pltpu.VMEM((HALO, Z, T), jnp.int32),
            vmem(6, HALO, Z, T),
            pltpu.VMEM((HALO, Z, T), jnp.int32),
            vmem(chunks, 6, nf * SUB, ways),
            vmem(chunks, 3, nf * SUB, ways),
            vmem(chunks, 3, nf * SUB, ways),
            vmem(chunks, 3, nf * SUB, ways),
            vmem(chunks, 6, nf * SUB, ways),
            dma(chunks, 2),
            dma(chunks, 2),
            dma(chunks, 2),
            dma(chunks, 2),
            dma(nl, 2, 2),
            dma(nl, 2, 2),
            dma(2),
            dma(2),
            dma(chunks, 5),
            dma(chunks, 3),
        ],
        compiler_params=pltpu.CompilerParams(
            vmem_limit_bytes=48 * 1024 * 1024, collective_id=0, has_side_effects=True
        ),
        name="fused",
    )(radius, state_start, state_section, phase, table)

    return pl.pallas_call(
        functools.partial(inverse_kernel, nf),
        out_shape=shape_of(6, R, Z, T),
        in_specs=[scalar] + [whole] * 4,
        out_specs=whole,
        compiler_params=pltpu.CompilerParams(vmem_limit_bytes=48 * 1024 * 1024),
        name="inverse",
    )(place, advanced, coef, weights, table)


def solution(mesh):
    in_specs = (
        P(None, "row", "gz", "theta"),
        P(None, "row", "gz", "theta"),
        P("row", "gz", "theta"),
        P(),
    )
    out_specs = P(None, "row", "gz", "theta")
    return jax.shard_map(shards, mesh=mesh, in_specs=in_specs, out_specs=out_specs, check_vma=False)
```

time: 59.4 us -> 39.3 us (0.66)
  starting transfers between devices: 18.8 us -> 0 us
  waiting for transfers between devices: 18.8 us -> 0 us
  Pallas kernels: 16.9 us -> 34.4 us
    ppermute x10 -> x0, starting transfers between devices: 18.8 us -> none  [the longest x1 6.21 us: shards(): lower = lax.ppermute(top, 'row', [(i, i + 1) for i in range(row_count - 1)])]
    ppermute x10 -> x0, waiting for transfers between devices: 18.8 us -> none  [the longest x4 9.8 us: along(): lax.ppermute(value, axis, [(i, (i + step) % count) for i in range(count)])]
    pallas_call x3 -> x1, Pallas kernels: 14.7 us -> 32.2 us  [shards(): pl.pallas_call(functools.partial(fused_kernel, nf, 2.0 * math.pi / length...]
    unnamed x14 -> x8, local copies, waits for them, and re-layouts: 3.35 us -> 3.7 us
  transfers between devices with their start and end apart: 10 -> 0, of which waited for: 6 -> 0; matrix products, arithmetic and copies ran while one was open for 2% -> 0% of each run, Pallas kernels for 13% -> 0%
where the time goes in v2:
time: 39.3 us; the launch traced here: 39.1 us
  Pallas kernels  34.4 us (88%)
  local copies, waits for them, and re-layouts  3.7 us (9%)
  other arithmetic  0.92 us (2%)
    pallas_call x1, Pallas kernels, shards(): pl.pallas_call(functools.partial(fused_kernel, nf, 2.0 * math.pi / length...  32.2 us
    unnamed x8, local copies, waits for them, and re-layouts  3.7 us
    pallas_call x1, Pallas kernels, shards(): pl.pallas_call(functools.partial(inverse_kernel, nf), out_shape=shape_of(...  2.21 us

profile of v2, /device:TPU:0, one launch (start us, length us, event | category | flops | bytes accessed | tf_op | source)
XLA Modules:
  0.0 39.1 jit_solution(8400655466846998631)
XLA Ops:
  0.0 0.1 add_convert_fusion.place
  0.1 0.0 copy-start.3
  0.1 0.6 %copy-done.3 = s32[4]{0:T(128)S(1)} copy-done((s32[4]{0:T(128)S(1)}, s32[4]{0:T(128)}, u32[]{:S(2)}) %copy-start.3) | copy-done | bytes 40
  0.7 0.1 fusion.8
  0.8 0.1 pad_maximum_fusion.1.weights
  0.9 0.6 %fusion.7 = (f32[256,64]{1,0:T(8,128)S(1)}, f32[256,64]{1,0:T(8,128)S(1)}) fusion(s32[256]{0:T(256)S(1)} %iota_add_fusion), kind=kLoop, calls=%fused_computation.11 | loop fusion | flops 229376 | bytes 132096 | tf_op jit(solution)/shard_map/cos | solution.py:471
  1.5 0.0 copy-start.2
  1.5 0.1 pad_maximum_fusion.table
  1.6 0.8 %copy-done.2 = s32[4,32,256]{2,1,0:T(8,128)S(1)} copy-done((s32[4,32,256]{2,1,0:T(8,128)S(1)}, s32[4,32,256]{2,1,0:T(8,128)}, u32[]{:S(2)}) %copy-start.2) | copy-done | bytes 131096
  2.4 0.0 copy-start
  2.4 1.1 %copy-done = f32[6,4,32,256]{3,2,1,0:T(8,128)S(1)} copy-done((f32[6,4,32,256]{3,2,1,0:T(8,128)S(1)}, f32[6,4,32,256]{3,2,1,0:T(8,128)}, u32[]{:S(2)}) %copy-start) | copy-done | bytes 786456
  3.5 0.0 copy-start.1
  3.5 1.1 %copy-done.1 = f32[6,4,32,256]{3,2,1,0:T(8,128)S(1)} copy-done((f32[6,4,32,256]{3,2,1,0:T(8,128)S(1)}, f32[6,4,32,256]{3,2,1,0:T(8,128)}, u32[]{:S(2)}) %copy-start.1) | copy-done | bytes 786456
  4.7 32.2 %fused.1 = (f32[6,4,32,256]{3,2,1,0:T(8,128)S(1)}, f32[4,6,32,128]{3,2,1,0:T(8,128)S(1)}) custom-call(f32[5]{0:T(128)S(1)} %add_convert_fusion.1.radius, f32[6,4,32,256]{3,2,1,0:T(8,128)S(1)} %copy-done, f32[6,4,32,256]{3,2,1,0:T(8,128)S(1)} %copy-done.1, s32[4,32,256]{2,1,0:T(8,128)S(1)} %copy-done.2, f32[256,128]{1,0:T(8,128)S(1)} %pad_maximum_fusion.table), custom_call_target="tpu_custom_call" | custom-call | tf_op jit(solution)/shard_map/fused/pallas_call | solution.py:514
  36.9 2.2 %inverse.1 = f32[6,4,32,256]{3,2,1,0:T(8,128)} custom-call(s32[2]{0:T(128)S(1)} %add_convert_fusion.place, f32[6,4,32,256]{3,2,1,0:T(8,128)S(1)} %get-tuple-element.7.adv, f32[4,6,32,128]{3,2,1,0:T(8,128)S(1)} %get-tuple-element.8.coef, f32[4,128]{1,0:T(4,128)S(1)} %pad_maximum_fusion.1.weights, f32[256,128]{1,0:T(8,128)S(1)} %pad_maximum_fusion.table), custom_call_target="tpu_custom_call" | custom-call | tf_op jit(solution)/shard_map/inverse/pallas_call | solution.py:552
  (3 shorter events, 0.0 us)
Async XLA Ops:
  0.1 0.7 %copy-start.3 = (s32[4]{0:T(128)S(1)}, s32[4]{0:T(128)}, u32[]{:S(2)}) copy-start(s32[4]{0:T(128)} %param.7) | copy-start | bytes 52
  1.5 0.9 %copy-start.2 = (s32[4,32,256]{2,1,0:T(8,128)S(1)}, s32[4,32,256]{2,1,0:T(8,128)}, u32[]{:S(2)}) copy-start(s32[4,32,256]{2,1,0:T(8,128)} %phase.1) | copy-start | bytes 393220
  2.4 1.1 %copy-start = (f32[6,4,32,256]{3,2,1,0:T(8,128)S(1)}, f32[6,4,32,256]{3,2,1,0:T(8,128)}, u32[]{:S(2)}) copy-start(f32[6,4,32,256]{3,2,1,0:T(8,128)} %start.1) | copy-start | bytes 2359300
  3.5 1.1 %copy-start.1 = (f32[6,4,32,256]{3,2,1,0:T(8,128)S(1)}, f32[6,4,32,256]{3,2,1,0:T(8,128)}, u32[]{:S(2)}) copy-start(f32[6,4,32,256]{3,2,1,0:T(8,128)} %sec.1) | copy-start | bytes 2359300

commit v3 on v2

--- a/solution.py
+++ b/solution.py
@@ -3,6 +3,7 @@
 
 import jax
 import jax.numpy as jnp
+import numpy as np
 from jax import lax
 from jax.experimental import pallas as pl
 from jax.experimental.pallas import tpu as pltpu
@@ -77,8 +78,8 @@
 
 
 def fused_kernel(
-    nf, angle_step, counts, radius, start, sec, phase, table, out, coef,
-    press, fz, zph, fe, tt, zt, lo, loph, hi, hiph, own, got, half, cross, whole_sum,
+    nf, length, counts, start_hbm, sec_hbm, phase_hbm, table_hbm, cutoff_hbm, out,
+    table, start, sec, phase, cutoff, in_sem, press, fz, zph, fe, tt, zt, lo, loph, hi, hiph, own, got, half, cross, whole_sum,
     lo_send, lo_recv, hi_send, hi_recv, z_send, z_recv, t_send, t_recv, c_send, c_recv,
 ):
     row_count, theta_count, gz_count = counts
@@ -89,6 +90,15 @@
     chunks = Z // SUB
     row = lax.axis_index("row")
     theta = lax.axis_index("theta")
+    take_phase = pltpu.make_async_copy(phase_hbm, phase, in_sem.at[0])
+    take_sec = pltpu.make_async_copy(sec_hbm, sec, in_sem.at[1])
+    take_start = pltpu.make_async_copy(start_hbm, start, in_sem.at[2])
+    take_table = pltpu.make_async_copy(table_hbm.at[pl.ds(theta * T, T)], table, in_sem.at[3])
+    take_cutoff = pltpu.make_async_copy(cutoff_hbm, cutoff, in_sem.at[4])
+    angle_step = 2.0 * math.pi / length
+    take_sec.start()
+    take_phase.start()
+    radius = [(row * R + i).astype(jnp.float32) for i in range(R + 1)]
     gz = lax.axis_index("gz")
     first = row == 0
     last = row == row_count - 1
@@ -160,6 +170,8 @@
         def _():
             start_all(mirrored(k))
 
+    take_sec.wait()
+    take_phase.wait()
     mirror_start(0)
 
     def upward_from(k):
@@ -210,6 +222,9 @@
         return out
 
     start_all(axial_copies())
+    take_start.start()
+    take_table.start()
+    take_cutoff.start()
 
     for r in range(R):
         press[r] = pressure_of([sec[c, r] for c in range(6)], phase[r])
@@ -268,14 +283,6 @@
         def _(k):
             theta_piece(lane, k)
 
-    for copy in theta_copies():
-        copy.wait()
-    for lane in range(NL // LANES):
-
-        @pl.loop(0, 2)
-        def _(k):
-            theta_piece(lane, k * (pieces - 1))
-
     for copy in axial_copies():
         copy.wait()
     for side, row0 in enumerate((0, SUB + Z)):
@@ -300,6 +307,15 @@
             for m in range(zstride):
                 zt[c, r, n, pl.ds(m, SUB, stride=zstride), :] = faces[m + 1] - faces[m]
 
+    for copy in theta_copies():
+        copy.wait()
+    for lane in range(NL // LANES):
+
+        @pl.loop(0, 2)
+        def _(k):
+            theta_piece(lane, k * (pieces - 1))
+
+    take_start.wait()
     for c in range(6):
         for n in range(NL // LANES):
             turned = jnp.transpose(tt[c, n])
@@ -316,6 +332,8 @@
                     tend = tend - sec[1, r] * sec[2, r] / (sec[0, r] * cell_radius)
                 out[c, r] = 0.75 * start[c, r] + 0.25 * (sec[c, r] + time_step * tend)
 
+    take_table.wait()
+    take_cutoff.wait()
     @pl.when(last)
     def _():
         for g in range(HALO):
@@ -386,7 +404,29 @@
         whole_sum[k, mine] = half[k] + cross[k]
         swap_back(k).start()
 
-    for k in range(chunks + 2):
+    ways = table.shape[1]
+    orders = lax.rem(lax.broadcasted_iota(jnp.int32, (SUB, ways), 1), ways // 2)
+    mode_scale = jnp.where(orders == 0, 1.0 / length, 2.0 / length)
+
+    def stage_d(k):
+        swap_back(k).wait()
+        kept = [jnp.where(orders <= cutoff[r], mode_scale, 0.0) for r in range(nf)]
+        rows = [
+            whole_sum[k, c, r * SUB : (r + 1) * SUB] * kept[r] for c in range(6) for r in range(nf)
+        ]
+        value = lax.dot_general(
+            jnp.concatenate(rows, 0),
+            table[...],
+            (((1,), (1,)), ((), ())),
+            preferred_element_type=jnp.float32,
+            precision=lax.Precision.HIGHEST,
+        )
+        for c in range(6):
+            for r in range(nf):
+                at = (c * nf + r) * SUB
+                out[c, r, k * SUB : (k + 1) * SUB] = value[at : at + SUB]
+
+    for k in range(chunks + 3):
         if k < chunks:
 
             @pl.when(first)
@@ -414,12 +454,8 @@
                 stage_b(k - 1)
             if 0 <= k - 2 < chunks:
                 stage_c(k - 2)
-
-    @pl.when(first)
-    def _():
-        for k in range(chunks):
-            swap_back(k).wait()
-            coef[k] = whole_sum[k]
+            if 0 <= k - 3:
+                stage_d(k - 3)
 
     for k in range(chunks):
 
@@ -434,49 +470,10 @@
                 copy.wait_send()
 
 
-def inverse_kernel(nf, place, adv, coef, weights, table, out):
-    _, R, Z, T = adv.shape
-    first = place[0] == 1
-
-    @pl.when(first)
-    def _():
-        for k in range(Z // SUB):
-            rows = [
-                coef[k, c, r * SUB : (r + 1) * SUB] * weights[r : r + 1] for c in range(6) for r in range(nf)
-            ]
-            value = lax.dot_general(
-                jnp.concatenate(rows, 0),
-                table[...],
-                (((1,), (1,)), ((), ())),
-                preferred_element_type=jnp.float32,
-                precision=lax.Precision.HIGHEST,
-            )
-            for c in range(6):
-                for r in range(nf):
-                    at = (c * nf + r) * SUB
-                    out[c, r, k * SUB : (k + 1) * SUB] = value[at : at + SUB]
-        for c in range(6):
-            for r in range(nf, R):
-                out[c, r] = adv[c, r]
-
-    @pl.when(jnp.logical_not(first))
-    def _():
-        out[...] = adv[...]
-
-
-def build_table(positions, mode_count, length):
-    orders = lax.iota(jnp.int32, mode_count)
-    phases = positions[:, None] * orders[None, :] % length
-    angles = phases.astype(jnp.float32) * (2.0 * math.pi / length)
-    return jnp.concatenate([jnp.cos(angles), jnp.sin(angles)], 1)
-
-
-def cycle_weights(cutoff, mode_count, length):
-    orders = lax.iota(jnp.int32, mode_count)
-    mode_scale = jnp.where(orders == 0, 1.0 / length, 2.0 / length)
-    kept_modes = orders[None, :] <= cutoff[:, None]
-    weight_half = jnp.where(kept_modes, mode_scale[None, :], 0.0)
-    return jnp.concatenate([weight_half, weight_half], 1)
+def full_table(mode_count, length):
+    phases = np.outer(np.arange(length), np.arange(mode_count)) % length
+    angles = phases * (2.0 * np.pi / length)
+    return np.concatenate([np.cos(angles), np.sin(angles)], 1).astype(np.float32)
 
 
 def shape_of(*dims):
@@ -485,9 +482,7 @@
 
 def shards(state_start, state_section, phase, cutoff):
     row_count = lax.axis_size("row")
-    row_id = lax.axis_index("row")
     theta_count = lax.axis_size("theta")
-    theta_id = lax.axis_index("theta")
     gz_count = lax.axis_size("gz")
     _, R, Z, T = state_section.shape
     NL = R * Z
@@ -496,13 +491,8 @@
     chunks = Z // SUB
     length = T * theta_count
     whole = pl.BlockSpec(memory_space=pltpu.VMEM)
-    scalar = pl.BlockSpec(memory_space=pltpu.SMEM)
-
-    radius = (row_id * R + lax.iota(jnp.int32, R + 1)).astype(jnp.float32)
-    place = jnp.stack([row_id == 0, row_id == row_count - 1]).astype(jnp.int32)
-    positions = theta_id * T + lax.iota(jnp.int32, T)
-    table = build_table(positions, KMODES, length)
-    weights = cycle_weights(cutoff, KMODES, length)
+
+    any_space = pl.BlockSpec(memory_space=pltpu.HBM)
     ways = 2 * KMODES
 
     def vmem(*dims):
@@ -511,12 +501,18 @@
     def dma(*dims):
         return pltpu.SemaphoreType.DMA(dims)
 
-    advanced, coef = pl.pallas_call(
-        functools.partial(fused_kernel, nf, 2.0 * math.pi / length, (row_count, theta_count, gz_count)),
-        out_shape=[shape_of(6, R, Z, T), shape_of(chunks, 6, nf * SUB, ways)],
-        in_specs=[scalar] + [whole] * 4,
-        out_specs=[whole] * 2,
+    return pl.pallas_call(
+        functools.partial(fused_kernel, nf, length, (row_count, theta_count, gz_count)),
+        out_shape=shape_of(6, R, Z, T),
+        in_specs=[any_space] * 5,
+        out_specs=whole,
         scratch_shapes=[
+            vmem(T, ways),
+            vmem(6, R, Z, T),
+            vmem(6, R, Z, T),
+            pltpu.VMEM((R, Z, T), jnp.int32),
+            pltpu.SMEM((nf,), jnp.int32),
+            dma(5),
             vmem(R, Z, T),
             vmem(7, R, nl, Z + 2 * SUB, LANES),
             pltpu.VMEM((R, nl, 2, SUB, LANES), jnp.int32),
@@ -544,19 +540,10 @@
             dma(chunks, 3),
         ],
         compiler_params=pltpu.CompilerParams(
-            vmem_limit_bytes=48 * 1024 * 1024, collective_id=0, has_side_effects=True
+            vmem_limit_bytes=65_500_000, collective_id=0, has_side_effects=True
         ),
         name="fused",
-    )(radius, state_start, state_section, phase, table)
-
-    return pl.pallas_call(
-        functools.partial(inverse_kernel, nf),
-        out_shape=shape_of(6, R, Z, T),
-        in_specs=[scalar] + [whole] * 4,
-        out_specs=whole,
-        compiler_params=pltpu.CompilerParams(vmem_limit_bytes=48 * 1024 * 1024),
-        name="inverse",
-    )(place, advanced, coef, weights, table)
+    )(state_start, state_section, phase, jnp.asarray(full_table(KMODES, length)), cutoff)
 
 
 def solution(mesh):

time: 39.3 us -> 36.8 us (0.936)
  local copies, waits for them, and re-layouts: 3.7 us -> 2.09 us
  other arithmetic: 0.92 us -> 0 us
    unnamed x8 -> x1, local copies, waits for them, and re-layouts: 3.7 us -> 2.09 us
    cos x1 -> x0, other arithmetic: 0.58 us -> none  [build_table(): return jnp.concatenate([jnp.cos(angles), jnp.sin(angles)], 1)]
    pallas_call x2 -> x1, Pallas kernels: 34.4 us -> 34.6 us  [shards(): pl.pallas_call(functools.partial(fused_kernel, nf, length, (row_count, th...]
where the time goes in v3:
time: 36.8 us; the launch traced here: 36.7 us
  Pallas kernels  34.6 us (94%)
  local copies, waits for them, and re-layouts  2.09 us (6%)
    pallas_call x1, Pallas kernels, shards(): pl.pallas_call(functools.partial(fused_kernel, nf, length, (row_count, th...  34.6 us
    unnamed x1, local copies, waits for them, and re-layouts  2.09 us

profile of v3, /device:TPU:0, one launch (start us, length us, event | category | flops | bytes accessed | tf_op | source)
XLA Modules:
  0.0 36.7 jit_solution(1396534789774294499)
XLA Ops:
  0.0 34.6 %fused.1 = f32[6,4,32,256]{3,2,1,0:T(8,128)} custom-call(f32[6,4,32,256]{3,2,1,0:T(8,128)} %start_hbm.1, f32[6,4,32,256]{3,2,1,0:T(8,128)} %sec_hbm.1, s32[4,32,256]{2,1,0:T(8,128)} %phase_hbm.1, f32[1024,128]{1,0:T(8,128)} %constant.2.clone.table_hbm, s32[4]{0:T(128)} %cutoff_hbm.1), custom_call_target="tpu_custom_call" | custom-call | tf_op jit(solution)/shard_map/fused/pallas_call | solution.py:504
  34.6 2.1 %copy.7 = f32[6,4,32,256]{3,2,1,0:T(8,128)} copy(f32[6,4,32,256]{3,2,1,0:T(8,128)} %fused.1) | data formatting | bytes 1572864
